TPU v7x, 32 devices: a whole 2x2x4 slice. The times are simulated.
32 devices in a mesh: tm: 8 (over y, x, core), space: 4 (over z).
Axes of the slice: x: 2, y: 2, z: 4, core: 2. Of those that a mesh axis runs over, the one named last changes fastest.
Arguments:
- trajectory: float32 [64, 256, 1024], P('tm', 'space'), may hold values from -1.2 to 1.2
- initial_state: float32 [256, 1024], P('space'), may hold values from -1 to 1
- residual: float32 [64, 256, 1024], P('tm', 'space'), may hold values from -3000 to 3000
- mobility: float32 [256, 1024], P('space'), may hold values from 20 to 200
Outputs:
- update: float32 [64, 256, 1024], P('tm', 'space')
- reduction: float32 [], replicated
All inputs are finite; a program needn't handle non-finite values.
Results may differ from a plain program's by a relative error of at most 0.00015.
Values sent between devices are 32-bit elements; how exact they have to be, the bound alone decides.
A program may use at most 64 MiB of HBM per device.

v0:
```python
import functools
import jax
import jax.numpy as jnp
from jax import lax
from jax.experimental import pallas as pl
from jax.experimental.pallas import tpu as pltpu
from jax.sharding import PartitionSpec as P

NT = 64
SWEEPS = 16


circ_weight = 0.2
time_step = 0.01
damping = 0.8
reaction_scale = 40.0


def padded_2(block, sides, width):
    for axis, dim in sides:
        count = lax.axis_size(axis)
        forward = [(i, i + 1) for i in range(count - 1)]
        forward.append((count - 1, 0))
        backward = [(target, source) for source, target in forward]
        low = lax.ppermute(
            lax.slice_in_dim(block, block.shape[dim] - width, None, axis=dim), axis, forward
        )
        high = lax.ppermute(lax.slice_in_dim(block, 0, width, axis=dim), axis, backward)
        block = jnp.concatenate([low, block, high], axis=dim)
    return block


def passed_along(block, axis, distance):
    devices = range(lax.axis_size(axis))
    route = [(i - distance, i) for i in devices if i - distance in devices]
    return lax.ppermute(block, axis, route)


def time_tables(step_count):
    positions = jnp.arange(step_count).astype(jnp.float32)
    pair_ids = jnp.arange(step_count // 2).astype(jnp.float32)
    phases = 2.0 * jnp.pi * pair_ids / step_count
    angles = phases[:, None] * positions[None, :]
    forward = jnp.stack([jnp.cos(angles), -jnp.sin(angles)], axis=1).reshape(step_count, step_count)
    row_id = jnp.arange(step_count)[:, None]
    forward = jnp.where(row_id == 1, jnp.cos(jnp.pi * positions)[None, :], forward)
    scaling = jnp.where(jnp.arange(step_count) < 2, 1.0, 2.0) / step_count
    inverse = forward.T * scaling[None, :]
    factor = circ_weight ** (1.0 / step_count)
    shift_pair = (1.0 - factor * jnp.cos(phases)) / time_step
    shifts = jnp.stack([shift_pair, shift_pair], axis=1).reshape(step_count)
    shifts = shifts.at[1].set((1.0 + factor) / time_step)
    coupling = factor * jnp.sin(phases) / time_step
    signed = jnp.stack([-coupling, coupling], axis=1).reshape(step_count)
    weights = circ_weight ** (positions / step_count)
    return (forward, inverse, shifts, signed, weights)


def neg_laplace(values):
    padded = padded_2(values, (("space", 1),), 1)
    middle = padded[:, 1:-1, :]
    neighbours = padded[:, 2:, :] + padded[:, :-2, :]
    neighbours = neighbours + jnp.roll(middle, 1, axis=2) + jnp.roll(middle, -1, axis=2)
    return 4.0 * values - neighbours


TILE = 8


def relax_kernel(
    count, shift_ref, signed_ref, spec_ref, base_ref, mob_ref, out_ref,
    state, gain, cross, start_val, sent, halo, send_sem, recv_sem,
):
    coefs, rows, cols = spec_ref.shape
    pairs, tiles = coefs // 2, rows // TILE
    keep = 1.0 - damping
    me = lax.axis_index("space")
    prev, after = lax.rem(me + count - 1, count), lax.rem(me + 1, count)

    barrier = pltpu.get_barrier_semaphore()
    for other in (prev, after):
        pl.semaphore_signal(
            barrier, inc=1, device_id={"space": other}, device_id_type=pl.DeviceIdType.MESH
        )
    pl.semaphore_wait(barrier, 2)

    def edge(slot, q, side):
        return pltpu.make_async_remote_copy(
            src_ref=sent.at[slot, q, side],
            dst_ref=halo.at[slot, q, 1 - side],
            send_sem=send_sem.at[slot, q, side],
            recv_sem=recv_sem.at[slot, q, 1 - side],
            device_id={"space": prev if side == 0 else after},
            device_id_type=pl.DeviceIdType.MESH,
        )

    def send(slot, q):
        for side in range(2):
            edge(slot, q, side).start()

    def prepare(q, _):
        sig_e, sig_o = shift_ref[2 * q], shift_ref[2 * q + 1]
        c_e = signed_ref[2 * q]
        for t in [0, tiles - 1] + list(range(1, tiles - 1)):
            span = pl.ds(t * TILE, TILE)
            mob, base = mob_ref[span, :], base_ref[span, :]
            d_e, d_o = sig_e + base, sig_o + base
            scale = damping / (d_e * d_o + c_e * c_e)
            s_e, s_o = spec_ref[2 * q, span, :], spec_ref[2 * q + 1, span, :]
            b_e = scale * (d_o * s_e - c_e * s_o)
            b_o = scale * (d_e * s_o + c_e * s_e)
            scaled = scale * mob
            gain[2 * q, span, :] = scaled * d_o
            gain[2 * q + 1, span, :] = scaled * d_e
            cross[q, span, :] = scaled * c_e
            start_val[2 * q, span, :] = b_e
            start_val[2 * q + 1, span, :] = b_o
            own = pl.ds((t + 1) * TILE, TILE)
            state[0, 2 * q, own, :] = b_e
            state[0, 2 * q + 1, own, :] = b_o
            if t == 0:
                sent[0, q, 0, 0:1, :] = b_e[0:1]
                sent[0, q, 0, 1:2, :] = b_o[0:1]
            if t == tiles - 1:
                sent[0, q, 1, 0:1, :] = b_e[TILE - 1 :]
                sent[0, q, 1, 1:2, :] = b_o[TILE - 1 :]
                send(0, q)
        return 0

    lax.fori_loop(0, pairs, prepare, 0)

    def around(slot, m, t):
        top = (t + 1) * TILE
        mid = state[slot, m, pl.ds(top, TILE), :]
        total = state[slot, m, pl.ds(top - 1, TILE), :] + state[slot, m, pl.ds(top + 1, TILE), :]
        total = total + (pltpu.roll(mid, 1, 1) + pltpu.roll(mid, cols - 1, 1))
        return mid, total

    def sweep(s, _):
        now = lax.rem(s, 2)
        later = 1 - now

        def one_pair(q, _):
            for side in range(2):
                edge(now, q, side).wait()
            for part in range(2):
                state[now, 2 * q + part, pl.ds(TILE - 1, 1), :] = halo[now, q, 0, part : part + 1, :]
                state[now, 2 * q + part, pl.ds(TILE + rows, 1), :] = halo[now, q, 1, part : part + 1, :]
            for t in [0, tiles - 1] + list(range(1, tiles - 1)):
                span = pl.ds(t * TILE, TILE)
                own = pl.ds((t + 1) * TILE, TILE)
                y_e, n_e = around(now, 2 * q, t)
                y_o, n_o = around(now, 2 * q + 1, t)
                c = cross[q, span, :]
                new_e = keep * y_e + start_val[2 * q, span, :] + (gain[2 * q, span, :] * n_e - c * n_o)
                new_o = keep * y_o + start_val[2 * q + 1, span, :] + (gain[2 * q + 1, span, :] * n_o + c * n_e)
                state[later, 2 * q, own, :] = new_e
                state[later, 2 * q + 1, own, :] = new_o
                if t == 0:
                    sent[later, q, 0, 0:1, :] = new_e[0:1]
                    sent[later, q, 0, 1:2, :] = new_o[0:1]
                if t == tiles - 1:
                    sent[later, q, 1, 0:1, :] = new_e[TILE - 1 :]
                    sent[later, q, 1, 1:2, :] = new_o[TILE - 1 :]

                    @pl.when(s < SWEEPS - 2)
                    def _():
                        send(later, q)

            return 0

        return lax.fori_loop(0, pairs, one_pair, 0)

    lax.fori_loop(0, SWEEPS - 1, sweep, 0)
    last = (SWEEPS - 1) % 2

    def store(m, _):
        out_ref[m] = state[last, m, TILE : TILE + rows, :]
        return 0

    lax.fori_loop(0, coefs, store, 0)


def relax_pairs(spectrum, shifts, signed, frozen, mobility):
    coefs, rows, cols = spectrum.shape
    pairs = coefs // 2
    count = lax.axis_size("space")
    vmem = pl.BlockSpec(memory_space=pltpu.VMEM)
    smem = pl.BlockSpec(memory_space=pltpu.SMEM)
    return pl.pallas_call(
        functools.partial(relax_kernel, count),
        out_shape=jax.ShapeDtypeStruct(spectrum.shape, jnp.float32),
        in_specs=[smem, smem, vmem, vmem, vmem],
        out_specs=vmem,
        scratch_shapes=[
            pltpu.VMEM((2, coefs, rows + 2 * TILE, cols), jnp.float32),
            pltpu.VMEM((coefs, rows, cols), jnp.float32),
            pltpu.VMEM((pairs, rows, cols), jnp.float32),
            pltpu.VMEM((coefs, rows, cols), jnp.float32),
            pltpu.VMEM((2, pairs, 2, 2, cols), jnp.float32),
            pltpu.VMEM((2, pairs, 2, 2, cols), jnp.float32),
            pltpu.SemaphoreType.DMA((2, pairs, 2)),
            pltpu.SemaphoreType.DMA((2, pairs, 2)),
        ],
        compiler_params=pltpu.CompilerParams(
            collective_id=0, has_side_effects=True, vmem_limit_bytes=32 * 1024 * 1024
        ),
    )(shifts, signed, spectrum, frozen + 4.0 * mobility, mobility)


def precondition(values, frozen, mobility, tables):
    forward, inverse, shifts, signed, weights = tables
    steps_dev = values.shape[0]
    time_rank = lax.axis_index("tm")
    offset = time_rank * steps_dev
    own_weights = lax.dynamic_slice_in_dim(weights, offset, steps_dev)
    own_shifts = lax.dynamic_slice_in_dim(shifts, offset, steps_dev)
    own_signed = lax.dynamic_slice_in_dim(signed, offset, steps_dev)
    weighted = own_weights[:, None, None] * values
    spectrum = jnp.einsum(
        "mj,jrc->mrc",
        forward,
        lax.all_to_all(weighted, "tm", split_axis=1, concat_axis=0, tiled=True),
        precision=lax.Precision.HIGHEST,
    )
    owned_part = lax.all_to_all(spectrum, "tm", split_axis=0, concat_axis=1, tiled=True)
    solved = relax_pairs(owned_part, own_shifts, own_signed, frozen, mobility)
    in_time = jnp.einsum(
        "jm,mrc->jrc",
        inverse,
        lax.all_to_all(solved, "tm", split_axis=1, concat_axis=0, tiled=True),
        precision=lax.Precision.HIGHEST,
    )
    restored = lax.all_to_all(in_time, "tm", split_axis=0, concat_axis=1, tiled=True)
    return restored / own_weights[:, None, None]


LANES = 128


def sum_kernel(t_count, z_count, x_ref, out_ref, t_got, z_own, z_got, t_send, t_recv, z_send, z_recv):
    barrier = pltpu.get_barrier_semaphore()
    places = (("tm", t_count), ("space", z_count))
    for axis, count in places:
        me = lax.axis_index(axis)
        for k in range(1, count):
            pl.semaphore_signal(
                barrier, inc=1, device_id={axis: lax.rem(me + k, count)},
                device_id_type=pl.DeviceIdType.MESH,
            )
    pl.semaphore_wait(barrier, t_count + z_count - 2)
    for axis, count, src, got, snd, rcv in (
        ("tm", t_count, x_ref, t_got, t_send, t_recv),
        ("space", z_count, z_own, z_got, z_send, z_recv),
    ):
        me = lax.axis_index(axis)
        made = []
        for k in range(1, count):
            made.append(
                pltpu.make_async_remote_copy(
                    src_ref=src, dst_ref=got.at[me], send_sem=snd.at[k], recv_sem=rcv.at[k],
                    device_id={axis: lax.rem(me + k, count)},
                    device_id_type=pl.DeviceIdType.MESH,
                )
            )
        for copy in made:
            copy.start()
        got[me] = src[...]
        for copy in made:
            copy.wait()
        total = got[0]
        for k in range(1, count):
            total = total + got[k]
        if axis == "tm":
            z_own[...] = total
        else:
            out_ref[...] = total


def summed(parts):
    t_count, z_count = lax.axis_size("tm"), lax.axis_size("space")
    row = lax.broadcasted_iota(jnp.int32, (TILE, LANES), 0)
    packed = jnp.zeros((TILE, LANES), jnp.float32)
    for k, part in enumerate(parts):
        packed = jnp.where(row == k, part, packed)
    vmem = pl.BlockSpec(memory_space=pltpu.VMEM)
    dma = pltpu.SemaphoreType.DMA
    total = pl.pallas_call(
        functools.partial(sum_kernel, t_count, z_count),
        out_shape=jax.ShapeDtypeStruct((TILE, LANES), jnp.float32),
        in_specs=[vmem],
        out_specs=vmem,
        scratch_shapes=[
            pltpu.VMEM((t_count, TILE, LANES), jnp.float32),
            pltpu.VMEM((TILE, LANES), jnp.float32),
            pltpu.VMEM((z_count, TILE, LANES), jnp.float32),
            dma((t_count,)), dma((t_count,)), dma((z_count,)), dma((z_count,)),
        ],
        compiler_params=pltpu.CompilerParams(
            collective_id=2, has_side_effects=True, vmem_limit_bytes=4 * 1024 * 1024
        ),
    )(packed)
    return [total[k, 0] for k in range(len(parts))]


def jacobian(values, trajectory, mobility):
    arriving = passed_along(values[-1:], "tm", 1)
    earlier = jnp.concatenate([arriving, values[:-1]], axis=0)
    reaction = reaction_scale * (3.0 * trajectory * trajectory - 1.0)
    return (values - earlier) / time_step + mobility[None] * neg_laplace(values) + reaction * values


def on_device(trajectory, initial_state, residual, mobility):
    tables = time_tables(NT)
    frozen = reaction_scale * jnp.maximum(3.0 * initial_state * initial_state - 1.0, 0.0)
    direction = precondition(residual, frozen, mobility, tables)
    applied = jacobian(direction, trajectory, mobility)
    norm_square, cross_sum, squared_applied = summed(
        (jnp.sum(residual * residual), jnp.sum(residual * applied), jnp.sum(applied * applied))
    )
    projection = cross_sum / norm_square
    squared_sum = squared_applied / norm_square
    remainder = jnp.maximum(squared_sum - projection * projection, 0.0)
    update = cross_sum / squared_applied * direction
    reduction = jnp.sqrt(remainder / squared_sum)
    return (update, reduction)


def solution(mesh):
    placed = (P("tm", "space", None), P("space", None), P("tm", "space", None), P("space", None))
    return jax.shard_map(
        on_device,
        mesh=mesh,
        in_specs=placed,
        out_specs=(P("tm", "space", None), P()),
        check_vma=False,
    )
```

profile of v0, /device:TPU:0, one launch (start us, length us, event | category | flops | bytes accessed | tf_op | source)
XLA Modules:
  0.0 246.3 jit_solution(15403682231192510077)
XLA Ops:
  0.7 0.1 dynamic_slice.11
  0.7 4.1 %copy_multiply_fusion = f32[8,64,1024]{2,0,1:T(8,128)} fusion(f32[8,64,1024]{2,1,0:T(8,128)} %param.8, f32[8]{0:T(128)S(1)} %dynamic_slice.11), kind=kLoop, calls=%fused_computation.26 | loop fusion | flops 524288 | bytes 4194336 | tf_op jit(solution)/shard_map/mul | solution.py:219
  4.9 5.2 %all-to-all-start = ((f32[8,64,1024]{2,0,1:T(8,128)}), f32[8,64,1024]{2,0,1:T(8,128)S(1)}, u32[]{:S(2)}, u32[]{:S(2)}) async-start(f32[8,64,1024]{2,0,1:T(8,128)} %copy_multiply_fusion), calls=%async_computation | async-start | bytes 4194304 | tf_op jit(solution)/shard_map/all_to_all | solution.py:223
  10.1 0.1 multiply_cosine_fusion
  10.3 0.1 pad_maximum_fusion.2
  10.4 26.3 %all-to-all-done = f32[8,64,1024]{2,0,1:T(8,128)S(1)} async-done(((f32[8,64,1024]{2,0,1:T(8,128)}), f32[8,64,1024]{2,0,1:T(8,128)S(1)}, u32[]{:S(2)}, u32[]{:S(2)}) %all-to-all-start) | async-done | bytes 2097184 | tf_op jit(solution)/shard_map/all_to_all | solution.py:223
  36.7 1.9 fusion.13
  38.6 2.5 %copy.72 = f32[64,8,1024]{2,1,0:T(8,128)} copy(f32[64,8,1024]{2,0,1:T(8,128)S(1)} %fusion.13) | data formatting | bytes 4194304 | tf_op jit(solution)/shard_map/mj,jrc->mrc/dot_general | solution.py:220
  41.2 3.7 %all-to-all-start.1 = ((f32[64,8,1024]{2,1,0:T(8,128)}), f32[64,8,1024]{2,1,0:T(8,128)S(1)}, u32[]{:S(2)}, u32[]{:S(2)}) async-start(f32[64,8,1024]{2,1,0:T(8,128)} %copy.72), calls=%async_computation.1 | async-start | bytes 4194304 | tf_op jit(solution)/shard_map/all_to_all | solution.py:226
  45.0 0.1 copy.68
  45.0 0.1 reshape.226
  45.2 0.1 dynamic_slice.10.signed_ref
  45.3 0.1 copy.67
  45.4 0.1 reshape.225
  45.5 0.1 dynamic_slice.9.shift_ref
  45.6 0.1 fusion.20.base_ref
  45.7 25.8 %all-to-all-done.1 = f32[64,8,1024]{2,1,0:T(8,128)S(1)} async-done(((f32[64,8,1024]{2,1,0:T(8,128)}), f32[64,8,1024]{2,1,0:T(8,128)S(1)}, u32[]{:S(2)}, u32[]{:S(2)}) %all-to-all-start.1) | async-done | bytes 2097184 | tf_op jit(solution)/shard_map/all_to_all | solution.py:226
  71.4 0.1 copy.99
  71.6 66.2 %shard_map.59 = f32[8,64,1024]{2,1,0:T(8,128)S(1)} custom-call(f32[8]{0:T(128)S(1)} %dynamic_slice.9.shift_ref, f32[8]{0:T(128)S(1)} %dynamic_slice.10.signed_ref, f32[8,64,1024]{2,1,0:T(8,128)S(1)} %bitcast.37, f32[64,1024]{1,0:T(8,128)S(1)} %fusion.20.base_ref, f32[64,1024]{1,0:T(8,128)S(1)} %copy-done), custom_call_target="tpu_custom_call" | custom-call | tf_op jit(solution)/shard_map/pallas_call | solution.py:190
  137.8 2.5 %copy.74 = f32[8,64,1024]{2,0,1:T(8,128)} copy(f32[8,64,1024]{2,1,0:T(8,128)S(1)} %shard_map.59) | data formatting | bytes 4194304 | tf_op jit(solution)/shard_map/pallas_call | solution.py:190
  140.3 3.6 %all-to-all-start.2 = ((f32[8,64,1024]{2,0,1:T(8,128)}), f32[8,64,1024]{2,0,1:T(8,128)S(1)}, u32[]{:S(2)}, u32[]{:S(2)}) async-start(f32[8,64,1024]{2,0,1:T(8,128)} %copy.74), calls=%async_computation.2 | async-start | bytes 4194304 | tf_op jit(solution)/shard_map/all_to_all | solution.py:231
  144.0 26.5 %all-to-all-done.2 = f32[8,64,1024]{2,0,1:T(8,128)S(1)} async-done(((f32[8,64,1024]{2,0,1:T(8,128)}), f32[8,64,1024]{2,0,1:T(8,128)S(1)}, u32[]{:S(2)}, u32[]{:S(2)}) %all-to-all-start.2) | async-done | bytes 2097184 | tf_op jit(solution)/shard_map/all_to_all | solution.py:231
  170.5 2.0 fusion.11
  172.5 2.5 %copy.77 = f32[64,8,1024]{2,1,0:T(8,128)} copy(f32[64,8,1024]{2,0,1:T(8,128)S(1)} %fusion.11) | data formatting | bytes 4194304 | tf_op jit(solution)/shard_map/jm,mrc->jrc/dot_general | solution.py:228
  175.0 4.7 %all-to-all-start.3 = ((f32[64,8,1024]{2,1,0:T(8,128)}), f32[64,8,1024]{2,1,0:T(8,128)}, u32[]{:S(2)}, u32[]{:S(2)}) async-start(f32[64,8,1024]{2,1,0:T(8,128)} %copy.77), calls=%async_computation.3 | async-start | bytes 4194304 | tf_op jit(solution)/shard_map/all_to_all | solution.py:234
  179.7 1.1 multiply_reduce_fusion
  180.8 0.6 compare_select_fusion
  181.5 24.6 %all-to-all-done.3 = f32[64,8,1024]{2,1,0:T(8,128)} async-done(((f32[64,8,1024]{2,1,0:T(8,128)}), f32[64,8,1024]{2,1,0:T(8,128)}, u32[]{:S(2)}, u32[]{:S(2)}) %all-to-all-start.3) | async-done | bytes 2097184 | tf_op jit(solution)/shard_map/all_to_all | solution.py:234
  206.1 2.8 %copy.78 = f32[8,8,8,1024]{3,1,2,0:T(8,128)S(1)} copy(f32[8,8,8,1024]{3,2,1,0:T(8,128)} %bitcast.13) | data formatting | bytes 4194304 | tf_op jit(solution)/shard_map/all_to_all | solution.py:234
  208.9 0.3 bitcast_divide_fusion
  209.2 0.3 slice.68
  209.5 0.0 copy-start.3
  209.5 0.8 fusion.30
  210.3 0.0 copy-start.2
  210.4 1.4 collective-permute-start
  211.9 2.1 collective-permute-start.1
  213.9 0.0 collective-permute-start.2
  213.9 0.1 fusion.31
  214.1 0.0 collective-permute-done
  214.1 0.3 copy.80
  214.4 1.6 collective-permute-done.1
  215.9 4.0 %collective-permute-done.2 = f32[8,1,1024]{2,0,1:T(8,128)S(1)} collective-permute-done((f32[8,1,1024]{2,0,1:T(8,128)S(1)}, f32[8,1,1024]{2,0,1:T(8,128)S(1)}, u32[]{:S(2)}, u32[]{:S(2)}) %collective-permute-start.2) | collective-permute-done | bytes 32800 | tf_op jit(solution)/shard_map/ppermute | solution.py:25
  220.0 6.8 %multiply_reduce_fusion.2 = (f32[]{:T(128)}, f32[]{:T(128)}) fusion(f32[8,64,1024]{2,1,0:T(8,128)S(1)} %copy-done.2, f32[8,64,1024]{2,0,1:T(8,128)S(1)} %bitcast_divide_fusion, f32[8,64,1024]{2,1,0:T(8,128)S(1)} %copy-done.3, f32[8,64,1]{2,0,1:T(8,128)S(1)} %get-tuple-element.26, f32[8,64,1023]{2,0,1:T(8,128)S(1)} %get-tuple-element.24, ...), kind=kLoop, calls=%fused_computation.25 | loop fusion | flops 12582910 | bytes 12910600 | tf_op jit(solution)/shard_map/reduce_sum | solution.py:319
  226.7 1.4 select_select_fusion.x_ref
  228.1 8.3 %shard_map.60 = f32[8,128]{1,0:T(8,128)S(1)} custom-call(f32[8,128]{1,0:T(8,128)S(1)} %select_select_fusion.x_ref), custom_call_target="tpu_custom_call" | custom-call | tf_op jit(solution)/shard_map/pallas_call | solution.py:288
  236.4 0.5 fusion.33
  242.3 0.3 broadcast_multiply_fusion
  242.6 2.5 %copy.84 = f32[8,64,1024]{2,1,0:T(8,128)} copy(f32[8,64,1024]{2,0,1:T(8,128)S(1)} %broadcast_multiply_fusion) | data formatting | bytes 4194304
  (25 shorter events, 0.3 us)
Async XLA Ops:
  4.9 31.8 %all-to-all-start = ((f32[8,64,1024]{2,0,1:T(8,128)}), f32[8,64,1024]{2,0,1:T(8,128)S(1)}, u32[]{:S(2)}, u32[]{:S(2)}) async-start(f32[8,64,1024]{2,0,1:T(8,128)} %copy_multiply_fusion), calls=%async_computation | async-start | bytes 4194304 | tf_op jit(solution)/shard_map/all_to_all | solution.py:223
  41.1 4.4 %copy-start = (f32[64,1024]{1,0:T(8,128)S(1)}, f32[64,1024]{1,0:T(8,128)}, u32[]{:S(2)}) copy-start(f32[64,1024]{1,0:T(8,128)} %mob_ref.1) | copy-start | bytes 786436
  41.2 4.4 %copy-start.4 = (f32[64,1024]{1,0:T(8,128)S(1)}, f32[64,1024]{1,0:T(8,128)}, u32[]{:S(2)}) copy-start(f32[64,1024]{1,0:T(8,128)} %param.7) | copy-start | bytes 786436
  41.2 30.3 %all-to-all-start.1 = ((f32[64,8,1024]{2,1,0:T(8,128)}), f32[64,8,1024]{2,1,0:T(8,128)S(1)}, u32[]{:S(2)}, u32[]{:S(2)}) async-start(f32[64,8,1024]{2,1,0:T(8,128)} %copy.72), calls=%async_computation.1 | async-start | bytes 4194304 | tf_op jit(solution)/shard_map/all_to_all | solution.py:226
  140.3 30.2 %all-to-all-start.2 = ((f32[8,64,1024]{2,0,1:T(8,128)}), f32[8,64,1024]{2,0,1:T(8,128)S(1)}, u32[]{:S(2)}, u32[]{:S(2)}) async-start(f32[8,64,1024]{2,0,1:T(8,128)} %copy.74), calls=%async_computation.2 | async-start | bytes 4194304 | tf_op jit(solution)/shard_map/all_to_all | solution.py:231
  175.0 4.7 %copy-start.1 = (f32[8,64,1024]{2,1,0:T(8,128)S(1)}, f32[8,64,1024]{2,1,0:T(8,128)}, u32[]{:S(2)}) copy-start(f32[8,64,1024]{2,1,0:T(8,128)} %param.8) | copy-start | bytes 6291460
  175.0 31.1 %all-to-all-start.3 = ((f32[64,8,1024]{2,1,0:T(8,128)}), f32[64,8,1024]{2,1,0:T(8,128)}, u32[]{:S(2)}, u32[]{:S(2)}) async-start(f32[64,8,1024]{2,1,0:T(8,128)} %copy.77), calls=%async_computation.3 | async-start | bytes 4194304 | tf_op jit(solution)/shard_map/all_to_all | solution.py:234
  209.5 10.5 %copy-start.3 = (f32[8,64,1024]{2,1,0:T(8,128)S(1)}, f32[8,64,1024]{2,1,0:T(8,128)}, u32[]{:S(2)}) copy-start(f32[8,64,1024]{2,1,0:T(8,128)} %param.6) | copy-start | bytes 6291460
  210.3 9.6 %copy-start.2 = (f32[8,64,1024]{2,1,0:T(8,128)S(1)}, f32[8,64,1024]{2,1,0:T(8,128)}, u32[]{:S(2)}) copy-start(f32[8,64,1024]{2,1,0:T(8,128)} %param.8) | copy-start | bytes 6291460
  210.4 3.7 %collective-permute-start = (f32[1,64,1024]{2,1,0:T(8,128)S(1)}, f32[1,64,1024]{2,1,0:T(8,128)S(1)}, u32[]{:S(2)}, u32[]{:S(2)}) collective-permute-start(f32[1,64,1024]{2,1,0:T(8,128)S(1)} %copy.79), channel_id=1, source_target_pairs={{0,4},{4,8},{8,12},{12,16},{16,20},{20,24},{24,28},{1,5},{5,9},{9,... | collective-permute-start | bytes 786440 | tf_op jit(solution)/shard_map/ppermute | solution.py:36
  211.9 4.1 %collective-permute-start.1 = (f32[8,1,1024]{2,0,1:T(8,128)S(1)}, f32[8,1,1024]{2,0,1:T(8,128)S(1)}, u32[]{:S(2)}, u32[]{:S(2)}) collective-permute-start(f32[8,1,1024]{2,0,1:T(8,128)S(1)} %get-tuple-element.28), channel_id=1, source_target_pairs={{1,0},{2,1},{3,2},{0,3},{5,4},{6,5},{7,6},{4,7},{9,8},{10,9},{11,1... | collective-permute-start | bytes 98312 | tf_op jit(solution)/shard_map/ppermute | solution.py:28
  213.9 6.0 %collective-permute-start.2 = (f32[8,1,1024]{2,0,1:T(8,128)S(1)}, f32[8,1,1024]{2,0,1:T(8,128)S(1)}, u32[]{:S(2)}, u32[]{:S(2)}) collective-permute-start(f32[8,1,1024]{2,0,1:T(8,128)S(1)} %get-tuple-element.29), channel_id=1, source_target_pairs={{0,1},{1,2},{2,3},{3,0},{4,5},{5,6},{6,7},{7,4},{8,9},{9,10},{10,1... | collective-permute-start | bytes 98312 | tf_op jit(solution)/shard_map/ppermute | solution.py:25
where the time goes:
time: 247 us; the launch traced here: 246 us
  waiting for transfers between devices  109 us (44%)
  Pallas kernels  74.5 us (30%)
  starting transfers between devices  20.7 us (8%)
  local copies, waits for them, and re-layouts  15.9 us (6%)
  other arithmetic  15.1 us (6%)
  between operations  7.39 us (3%)
  matrix products  3.9 us (2%)
    pallas_call x1, Pallas kernels, relax_pairs(): pl.pallas_call(functools.partial(relax_kernel, count), out_shape=jax.Shap...  66.2 us
    all_to_all x1, waiting for transfers between devices, precondition(): lax.all_to_all(solved, 'tm', split_axis=1, concat_axis=0, tiled=True)  26.5 us
    all_to_all x1, waiting for transfers between devices, precondition(): lax.all_to_all(weighted, 'tm', split_axis=1, concat_axis=0, tiled=True)  26.3 us
    all_to_all x1, waiting for transfers between devices, precondition(): lax.all_to_all(spectrum, 'tm', split_axis=0, concat_axis=1, tiled=True)  25.8 us
    all_to_all x1, waiting for transfers between devices, precondition(): lax.all_to_all(in_time, 'tm', split_axis=0, concat_axis=1, tiled=True)  24.6 us
    pallas_call x1, Pallas kernels, summed(): pl.pallas_call(functools.partial(sum_kernel, t_count, z_count), out_shape...  8.27 us
    reduce_sum x1, other arithmetic, on_device(): jnp.sum(applied * applied)  6.76 us
    all_to_all x1, starting transfers between devices, precondition(): lax.all_to_all(weighted, 'tm', split_axis=1, concat_axis=0, tiled=True)  5.2 us
  transfers between devices with their start and end apart: 7, of which 6 were waited for; matrix products, arithmetic and copies ran while one was open for 1% of the time, Pallas kernels for 0%

commit v1 on v0

v1 whole, which is shorter than its diff:
```python
import functools
import math
import numpy as np
import jax
import jax.numpy as jnp
from jax import lax
from jax.experimental import pallas as pl
from jax.experimental.pallas import tpu as pltpu
from jax.sharding import PartitionSpec as P

SWEEPS = 16
SUB = 8
LANES = 128

circ_weight = 0.2
time_step = 0.01
damping = 0.8
reaction_scale = 40.0

MESH = pl.DeviceIdType.MESH
HIGHEST = lax.Precision.HIGHEST


def time_tables(count):
    f32 = np.float32
    positions = np.arange(count, dtype=f32)
    pair_ids = np.arange(count // 2, dtype=f32)
    phases = f32(2.0 * np.pi) * pair_ids / f32(count)
    angles = phases[:, None] * positions[None, :]
    forward = np.stack([np.cos(angles), -np.sin(angles)], axis=1).reshape(count, count)
    forward[1] = np.cos(f32(np.pi) * positions)
    inverse = forward.T * np.where(np.arange(count) < 2, f32(1.0), f32(2.0)) / f32(count)
    factor = circ_weight ** (1.0 / count)
    shifts = np.repeat((1.0 - factor * np.cos(phases)) / time_step, 2)
    shifts[1] = (1.0 + factor) / time_step
    coupling = factor * np.sin(phases) / time_step
    weights = circ_weight ** (np.arange(count) / count)
    order = np.arange(count).reshape(-1, SUB, 2).transpose(0, 2, 1).reshape(count)
    forward = (forward * weights[None, :])[order]
    inverse = (inverse / weights[:, None])[:, order]
    tiles = np.stack(
        [shifts[0::2].reshape(-1, SUB), shifts[1::2].reshape(-1, SUB), -coupling.reshape(-1, SUB)], axis=1
    )
    tiles = np.broadcast_to(tiles[..., None], tiles.shape + (LANES,))
    return forward.astype(f32), inverse.astype(f32), np.ascontiguousarray(tiles, dtype=f32)


class Plan:
    def __init__(self, t_count, z_count, steps, rows, cols, split):
        self.t, self.z = t_count, z_count
        self.k, self.rows, self.cols = steps, rows, cols
        self.q = split
        self.blocks = t_count // split
        self.r, self.c = rows * split // t_count, cols // split
        outer = 1 << (int(math.log2(t_count)) // 2)
        while self.blocks % outer:
            outer //= 2
        self.inner = self.blocks // outer

    def block_of(self, i, z):
        span = self.q * self.inner
        o, h, n = i // span, (i // self.inner) % self.q, i % self.inner
        b = o * self.inner + n + (o % 2) * (self.inner - 1 - 2 * n)
        return b + (z % 2) * (self.blocks - 1 - 2 * b), h

    def device_of(self, b, h, z):
        b = b + (z % 2) * (self.blocks - 1 - 2 * b)
        o, n = b // self.inner, b % self.inner
        n = n + (o % 2) * (self.inner - 1 - 2 * n)
        return o * self.q * self.inner + h * self.inner + n

    def row_neighbour(self, b, h, z, step):
        total = self.blocks * self.z
        g = (z * self.blocks + b + step + total) % total
        z2, b2 = g // self.blocks, g % self.blocks
        return {"tm": self.device_of(b2, h, z2), "space": z2}


def fold(v):
    total = v[:, :LANES]
    for i in range(1, v.shape[1] // LANES):
        total = total + v[:, i * LANES : (i + 1) * LANES]
    return total


def step_kernel(
    plan, phi_ref, psi_ref, tab_ref, x_ref, traj_ref, base_ref, mob_ref, dir_ref, sums_ref,
    got, y, gain, cross, start, out, prev, z_out, z_got, base_loc, mob_loc, t_got, z_own, zs_got,
    col_out, col_got,
    in_send, in_recv, row_send, row_recv, col_send, col_recv, back_send, back_recv, prev_send, prev_recv,
    edge_send, edge_recv, t_send, t_recv, z_send, z_recv,
):
    K, R, C, Q, T, Z = plan.k, plan.r, plan.c, plan.q, plan.t, plan.z
    NT, CT = K * T, C // LANES
    G = NT // (2 * SUB)
    rows, cols = plan.rows, plan.cols
    keep = 1.0 - damping
    me, z = lax.axis_index("tm"), lax.axis_index("space")
    b, h = plan.block_of(me, z)
    up, down = plan.row_neighbour(b, h, z, -1), plan.row_neighbour(b, h, z, 1)
    left = {"tm": plan.device_of(b, (h + Q - 1) % Q, z)}
    right = {"tm": plan.device_of(b, (h + 1) % Q, z)}
    region = b * Q + h

    barrier = pltpu.get_barrier_semaphore()
    for i in range(1, T):
        pl.semaphore_signal(barrier, inc=1, device_id={"tm": (me + i) % T}, device_id_type=MESH)
    for i in range(1, Z):
        pl.semaphore_signal(barrier, inc=1, device_id={"space": (z + i) % Z}, device_id_type=MESH)
    pl.semaphore_wait(barrier, T + Z - 2)

    def rows_of(blk):
        return pl.ds(pl.multiple_of(blk * R, SUB), R)

    def cols_of(part):
        return pl.ds(pl.multiple_of(part * C, LANES), C)

    def lane_tile(part, j):
        return pl.ds(pl.multiple_of(part * C + j * LANES, LANES), LANES)

    def sent_in(j, i):
        g = (region + i) % T
        gb, gh = g // Q, g % Q
        return pltpu.make_async_remote_copy(
            src_ref=x_ref.at[:, rows_of(gb), lane_tile(gh, j)],
            dst_ref=got.at[j, pl.ds(me * K, K)],
            send_sem=in_send.at[j, i], recv_sem=in_recv.at[j, i],
            device_id={"tm": plan.device_of(gb, gh, z)}, device_id_type=MESH,
        )

    def send_in(j, _):
        for i in range(1, T):
            sent_in(j, i).start()
        return 0

    lax.fori_loop(0, CT, send_in, 0)
    for j in range(CT):
        got[j, pl.ds(me * K, K)] = x_ref[:, rows_of(b), lane_tile(h, j)]
    base_loc[...] = base_ref[rows_of(b), cols_of(h)]
    mob_loc[...] = mob_ref[rows_of(b), cols_of(h)]

    flat = got.reshape(CT, NT * R, LANES)
    WIDE = 2 if CT % 2 == 0 else 1
    CH = WIDE * LANES

    def transform(j, _):
        span = pl.ds(pl.multiple_of(j * CH, LANES), CH)
        for w in range(WIDE):
            for i in range(1, T):
                sent_in(j * WIDE + w, i).wait()
        for r in range(R):
            steps = [flat[j * WIDE + w, pl.ds(r, NT, stride=R), :] for w in range(WIDE)]
            spec = jnp.dot(
                phi_ref[...], jnp.concatenate(steps, axis=1),
                precision=HIGHEST, preferred_element_type=jnp.float32,
            )
            base, mob = base_loc[r : r + 1, span], mob_loc[r : r + 1, span]
            for q in range(G):
                e, o = 2 * SUB * q, 2 * SUB * q + SUB
                s_e, s_o = spec[e : e + SUB], spec[o : o + SUB]
                wide = lambda k: jnp.tile(tab_ref[q, k], (1, CH // LANES))
                d_e, d_o, c = wide(0) + base, wide(1) + base, wide(2)
                scale = damping / (d_e * d_o + c * c)
                b_e = scale * (d_o * s_e - c * s_o)
                b_o = scale * (d_e * s_o + c * s_e)
                scaled = scale * mob
                gain[r, e : e + SUB, span] = scaled * d_o
                gain[r, o : o + SUB, span] = scaled * d_e
                cross[r, q * SUB : (q + 1) * SUB, span] = scaled * c
                start[r, e : e + SUB, span] = b_e
                start[r, o : o + SUB, span] = b_o
                y[0, r + 1, e : e + SUB, span] = b_e
                y[0, r + 1, o : o + SUB, span] = b_o
        return 0

    lax.fori_loop(0, CT // WIDE, transform, 0)

    def tile_of(q):
        return pl.ds(pl.multiple_of(q * 2 * SUB, 2 * SUB), 2 * SUB)

    def row_edge(slot, q, side):
        return pltpu.make_async_remote_copy(
            src_ref=y.at[slot, 1 if side == 0 else R, tile_of(q)],
            dst_ref=y.at[slot, R + 1 if side == 0 else 0, tile_of(q)],
            send_sem=row_send.at[slot, q, side], recv_sem=row_recv.at[slot, q, 1 - side],
            device_id=up if side == 0 else down, device_id_type=MESH,
        )

    def col_edge(slot, q, side):
        return pltpu.make_async_remote_copy(
            src_ref=col_out.at[slot, q, side], dst_ref=col_got.at[slot, q, 1 - side],
            send_sem=col_send.at[slot, q, side], recv_sem=col_recv.at[slot, q, 1 - side],
            device_id=left if side == 0 else right, device_id_type=MESH,
        )

    lane = lax.broadcasted_iota(jnp.int32, (SUB, LANES), 1)

    def packed(total, v, r, side):
        if side == 0:
            v, at = v[:, :LANES], 0
        else:
            v, at = v[:, C - LANES :], LANES - 1
        v = pltpu.roll(v, (r - at) % LANES, 1)
        return jnp.where(lane == r, v, total)

    def start_edges(slot, q):
        for side in range(2):
            row_edge(slot, q, side).start()
            if Q > 1:
                col_edge(slot, q, side).start()

    order = [0, R - 1] + list(range(1, R - 1))

    def first_edges(q, _):
        if Q > 1:
            for part in range(2):
                tile = pl.ds(pl.multiple_of(q * 2 * SUB, SUB) + part * SUB, SUB)
                lo = hi = jnp.zeros((SUB, LANES), jnp.float32)
                for r in range(R):
                    v = y[0, r + 1, tile, :]
                    lo, hi = packed(lo, v, r, 0), packed(hi, v, r, 1)
                col_out[0, q, 0, part] = lo
                col_out[0, q, 1, part] = hi
        start_edges(0, q)
        return 0

    lax.fori_loop(0, G, first_edges, 0)

    def sweep(s, _):
        now = lax.rem(s, 2)
        later = 1 - now

        def one(q, _):
            for side in range(2):
                row_edge(now, q, side).wait()
                if Q > 1:
                    col_edge(now, q, side).wait()
            e_at = pl.multiple_of(q * 2 * SUB, 2 * SUB)
            tiles = (pl.ds(e_at, SUB), pl.ds(e_at + SUB, SUB))
            c_tile = pl.ds(pl.multiple_of(q * SUB, SUB), SUB)
            ends = [[jnp.zeros((SUB, LANES), jnp.float32)] * 2 for _ in range(2)]

            def around(r, part):
                mid = y[now, r + 1, tiles[part], :]
                total = y[now, r, tiles[part], :] + y[now, r + 2, tiles[part], :]
                low, high = pltpu.roll(mid, 1, 1), pltpu.roll(mid, C - 1, 1)
                if Q > 1:
                    shift = lambda side, at: pltpu.roll(col_got[now, q, side, part], (at - r) % LANES, 1)
                    head = jnp.where(lane == 0, shift(0, 0), low[:, :LANES])
                    tail = jnp.where(lane == LANES - 1, shift(1, LANES - 1), high[:, C - LANES :])
                    low = jnp.concatenate([head, low[:, LANES:]], axis=1)
                    high = jnp.concatenate([high[:, : C - LANES], tail], axis=1)
                return mid, total + (low + high)

            for n, r in enumerate(order):
                y_e, n_e = around(r, 0)
                y_o, n_o = around(r, 1)
                c = cross[r, c_tile, :]
                new_e = keep * y_e + start[r, tiles[0], :] + (gain[r, tiles[0], :] * n_e - c * n_o)
                new_o = keep * y_o + start[r, tiles[1], :] + (gain[r, tiles[1], :] * n_o + c * n_e)
                y[later, r + 1, tiles[0], :] = new_e
                y[later, r + 1, tiles[1], :] = new_o
                if Q > 1:
                    for part, new in enumerate((new_e, new_o)):
                        for side in range(2):
                            ends[part][side] = packed(ends[part][side], new, r, side)
                if n == 1:

                    @pl.when(s < SWEEPS - 2)
                    def _():
                        for side in range(2):
                            row_edge(later, q, side).start()

            if Q > 1:
                for part in range(2):
                    for side in range(2):
                        col_out[later, q, side, part] = ends[part][side]

                @pl.when(s < SWEEPS - 2)
                def _():
                    for side in range(2):
                        col_edge(later, q, side).start()

            return 0

        return lax.fori_loop(0, G, one, 0)

    lax.fori_loop(0, SWEEPS - 1, sweep, 0)
    last = (SWEEPS - 1) % 2

    flat_out = out.reshape(CT, NT * R, LANES)

    def sent_back(j, i):
        g = (me + i) % T
        return pltpu.make_async_remote_copy(
            src_ref=out.at[j, pl.ds(g * K, K)], dst_ref=dir_ref.at[:, rows_of(b), lane_tile(h, j)],
            send_sem=back_send.at[j, i], recv_sem=back_recv.at[j, i],
            device_id={"tm": g}, device_id_type=MESH,
        )

    def sent_prev(j, i):
        g = (me + i) % T
        return pltpu.make_async_remote_copy(
            src_ref=out.at[j, (g * K + NT - 1) % NT], dst_ref=prev.at[rows_of(b), lane_tile(h, j)],
            send_sem=prev_send.at[j, i], recv_sem=prev_recv.at[j, i],
            device_id={"tm": g}, device_id_type=MESH,
        )

    def restore(j, _):
        span = pl.ds(pl.multiple_of(j * CH, LANES), CH)
        for r in range(R):
            steps = jnp.dot(
                psi_ref[...], y[last, r + 1, :, span],
                precision=HIGHEST, preferred_element_type=jnp.float32,
            )
            for w in range(WIDE):
                flat_out[j * WIDE + w, pl.ds(r, NT, stride=R), :] = steps[:, w * LANES : (w + 1) * LANES]
        for w in range(WIDE):
            for i in range(1, T):
                sent_back(j * WIDE + w, i).start()
                sent_prev(j * WIDE + w, i).start()
        return 0

    lax.fori_loop(0, CT // WIDE, restore, 0)
    for j in range(CT):
        dir_ref[:, rows_of(b), lane_tile(h, j)] = out[j, pl.ds(me * K, K)]
        prev[rows_of(b), lane_tile(h, j)] = out[j, (me * K + NT - 1) % NT]

    def arrive(j, _):
        for i in range(1, T):
            sent_back(j, i).wait()
            sent_prev(j, i).wait()
        return 0

    lax.fori_loop(0, CT, arrive, 0)

    for k in range(K):
        z_out[0, k : k + 1, :] = dir_ref[k, 0:1, :]
        z_out[1, k : k + 1, :] = dir_ref[k, rows - 1 : rows, :]
    edges = []
    for side in range(2):
        edges.append(
            pltpu.make_async_remote_copy(
                src_ref=z_out.at[side], dst_ref=z_got.at[1 - side],
                send_sem=edge_send.at[side], recv_sem=edge_recv.at[1 - side],
                device_id={"space": (z + (Z - 1 if side == 0 else 1)) % Z}, device_id_type=MESH,
            )
        )
    for copy in edges:
        copy.start()
    sub = lax.broadcasted_iota(jnp.int32, (SUB, cols), 0)
    has_prev = jnp.minimum(me, 1).astype(jnp.float32)
    tiles = rows // SUB

    def tile_sums(k, first, t, acc):
        span = pl.ds(t * SUB, SUB)
        v = dir_ref[k, span, :]
        if t == 0:
            above = jnp.where(sub == 0, z_got[0, pl.ds(k, 1), :], pltpu.roll(v, 1, 0))
        else:
            above = dir_ref[k, pl.ds(t * SUB - 1, SUB), :]
        if t == tiles - 1:
            below = jnp.where(sub == SUB - 1, z_got[1, pl.ds(k, 1), :], pltpu.roll(v, SUB - 1, 0))
        else:
            below = dir_ref[k, pl.ds(t * SUB + 1, SUB), :]
        near = above + below + (pltpu.roll(v, 1, 1) + pltpu.roll(v, cols - 1, 1))
        before = prev[span, :] * has_prev if first else dir_ref[k - 1, span, :]
        u = traj_ref[k, span, :]
        applied = (v - before) * (1.0 / time_step) + mob_ref[span, :] * (4.0 * v - near)
        applied = applied + reaction_scale * (3.0 * u * u - 1.0) * v
        res = x_ref[k, span, :]
        return acc[0] + fold(res * res), acc[1] + fold(res * applied), acc[2] + fold(applied * applied)

    zero = jnp.zeros((SUB, LANES), jnp.float32)
    acc = (zero, zero, zero)

    def some(k, first, which, acc):
        for t in which:
            acc = tile_sums(k, first, t, acc)
        return acc

    inner = list(range(1, tiles - 1))
    acc = some(0, True, inner, acc)
    acc = lax.fori_loop(1, K, lambda k, a: some(k, False, inner, a), acc)
    for copy in edges:
        copy.wait()
    acc = some(0, True, [0, tiles - 1], acc)
    acc = lax.fori_loop(1, K, lambda k, a: some(k, False, [0, tiles - 1], a), acc)

    row = lax.broadcasted_iota(jnp.int32, (SUB, LANES), 0)
    pack = zero
    for n in range(3):
        pack = jnp.where(row == n, jnp.sum(acc[n], axis=0, keepdims=True), pack)
    t_got[me] = pack
    z_own[...] = pack

    def exchange(axis, count, at, src, dst, snd, rcv):
        copies = []
        for i in range(1, count):
            copies.append(
                pltpu.make_async_remote_copy(
                    src_ref=src, dst_ref=dst.at[at], send_sem=snd.at[i], recv_sem=rcv.at[i],
                    device_id={axis: (at + i) % count}, device_id_type=MESH,
                )
            )
        for copy in copies:
            copy.start()
        for copy in copies:
            copy.wait()
        total = dst[0]
        for i in range(1, count):
            total = total + dst[i]
        return total

    part = exchange("tm", T, me, z_own.at[...], t_got, t_send, t_recv)
    z_own[...] = part
    zs_got[z] = part
    sums_ref[...] = exchange("space", Z, z, z_own.at[...], zs_got, z_send, z_recv)


def finish_kernel(sums_ref, dir_ref, out_ref, red_ref):
    sums = jnp.sum(sums_ref[...], axis=1, keepdims=True)
    norm, crossed, squared = sums[0:1], sums[1:2], sums[2:3]
    out_ref[...] = (crossed / squared)[None] * dir_ref[...]
    projection, squared_sum = crossed / norm, squared / norm
    remainder = jnp.maximum(squared_sum - projection * projection, 0.0)
    red_ref[...] = jnp.sqrt(remainder / squared_sum)


def column_split(t_count, rows):
    return max(1, t_count * SUB // rows)


def on_device(trajectory, initial_state, residual, mobility):
    t_count, z_count = lax.axis_size("tm"), lax.axis_size("space")
    steps, rows, cols = residual.shape
    plan = Plan(t_count, z_count, steps, rows, cols, column_split(t_count, rows))
    count = steps * t_count
    groups = count // (2 * SUB)
    forward, inverse, tables = time_tables(count)
    frozen = reaction_scale * jnp.maximum(3.0 * initial_state * initial_state - 1.0, 0.0)
    R, C, tiles = plan.r, plan.c, plan.c // LANES
    f32 = jnp.float32
    vmem = pl.BlockSpec(memory_space=pltpu.VMEM)
    dma = pltpu.SemaphoreType.DMA
    V = lambda *shape: pltpu.VMEM(shape, f32)
    direction, sums = pl.pallas_call(
        functools.partial(step_kernel, plan),
        out_shape=[jax.ShapeDtypeStruct(residual.shape, f32), jax.ShapeDtypeStruct((SUB, LANES), f32)],
        in_specs=[vmem] * 7,
        out_specs=[vmem, vmem],
        scratch_shapes=[
            V(tiles, count, R, LANES), V(2, R + 2, count, C), V(R, count, C), V(R, count // 2, C), V(R, count, C),
            V(tiles, count, R, LANES), V(rows, cols), V(2, steps, cols), V(2, steps, cols), V(R, C), V(R, C),
            V(t_count, SUB, LANES), V(SUB, LANES), V(z_count, SUB, LANES),
            V(2, groups, 2, 2, SUB, LANES), V(2, groups, 2, 2, SUB, LANES),
            dma((tiles, t_count)), dma((tiles, t_count)), dma((2, groups, 2)), dma((2, groups, 2)),
            dma((2, groups, 2)), dma((2, groups, 2)), dma((tiles, t_count)), dma((tiles, t_count)),
            dma((tiles, t_count)), dma((tiles, t_count)), dma((2,)), dma((2,)),
            dma((t_count,)), dma((t_count,)), dma((z_count,)), dma((z_count,)),
        ],
        compiler_params=pltpu.CompilerParams(
            collective_id=0, has_side_effects=True, vmem_limit_bytes=48 * 1024 * 1024
        ),
    )(jnp.asarray(forward), jnp.asarray(inverse), jnp.asarray(tables), residual, trajectory, frozen + 4.0 * mobility, mobility)
    update, reduction = pl.pallas_call(
        finish_kernel,
        grid=(steps,),
        out_shape=[jax.ShapeDtypeStruct(residual.shape, f32), jax.ShapeDtypeStruct((1, 1), f32)],
        in_specs=[
            pl.BlockSpec((SUB, LANES), lambda i: (0, 0)),
            pl.BlockSpec((1, rows, cols), lambda i: (i, 0, 0)),
        ],
        out_specs=[
            pl.BlockSpec((1, rows, cols), lambda i: (i, 0, 0)),
            pl.BlockSpec((1, 1), lambda i: (0, 0)),
        ],
    )(sums, direction)
    return (update, reduction[0, 0])


def solution(mesh):
    placed = (P("tm", "space", None), P("space", None), P("tm", "space", None), P("space", None))
    return jax.shard_map(
        on_device,
        mesh=mesh,
        in_specs=placed,
        out_specs=(P("tm", "space", None), P()),
        check_vma=False,
    )
```

time: 247 us -> 179 us (0.72)
  waiting for transfers between devices: 109 us -> 0 us
  Pallas kernels: 74.5 us -> 170 us
  starting transfers between devices: 20.7 us -> 0 us
  other arithmetic: 15.1 us -> 1.1 us
  local copies, waits for them, and re-layouts: 15.9 us -> 6.78 us
  between operations: 7.39 us -> 0.66 us
  matrix products: 3.9 us -> 0 us
    all_to_all x4 -> x0, waiting for transfers between devices: 103 us -> none  [the longest x1 26.5 us: precondition(): lax.all_to_all(solved, 'tm', split_axis=1, concat_axis=0, tiled=True)]
    pallas_call x2, Pallas kernels: 74.5 us -> 170 us  [the longest x1 164 us: on_device(): pl.pallas_call(functools.partial(step_kernel, plan), out_shape=[jax.Shape...]
    all_to_all x4 -> x0, starting transfers between devices: 17.2 us -> none  [the longest x1 5.2 us: precondition(): lax.all_to_all(weighted, 'tm', split_axis=1, concat_axis=0, tiled=True)]
    reduce_sum x2 -> x0, other arithmetic: 7.89 us -> none  [the longest x1 6.76 us: on_device(): jnp.sum(applied * applied)]
    ppermute x3 -> x0, waiting for transfers between devices: 5.59 us -> none  [the longest x1 4.03 us: padded_2(): lax.ppermute(lax.slice_in_dim(block, block.shape[dim] - width, None, axis...]
    dot_general x2 -> x0, local copies, waits for them, and re-layouts: 5.07 us -> none  [the longest x1 2.54 us: precondition(): jnp.einsum('mj,jrc->mrc', forward, lax.all_to_all(weighted, 'tm', split_a...]
    mul x2 -> x0, other arithmetic: 4.45 us -> none  [the longest x1 4.13 us: precondition(): weighted = own_weights[:, None, None] * values]
    unnamed x11 -> x14, local copies, waits for them, and re-layouts: 2.56 us -> 6.78 us
  transfers between devices with their start and end apart: 7 -> 0, of which waited for: 6 -> 0; matrix products, arithmetic and copies ran while one was open for 1% -> 0% of each run, Pallas kernels for 0% -> 0%
where the time goes in v1:
time: 179 us
  Pallas kernels  170 us (95%)
  local copies, waits for them, and re-layouts  6.78 us (4%)
    pallas_call x1, Pallas kernels, on_device(): pl.pallas_call(functools.partial(step_kernel, plan), out_shape=[jax.Shape...  164 us
    unnamed x14, local copies, waits for them, and re-layouts  6.78 us
    pallas_call x1, Pallas kernels, on_device(): pl.pallas_call(finish_kernel, grid=(steps,), out_shape=[jax.ShapeDtypeStr...  6.06 us

profile of v1, /device:TPU:0, one launch (start us, length us, event | category | flops | bytes accessed | tf_op | source)
XLA Modules:
  0.0 178.7 jit_solution(3990032788381472201)
XLA Ops:
  0.6 1.1 fusion.3.base_ref
  1.7 0.0 copy-start
  1.7 1.6 copy-done
  3.3 0.0 copy-start.2
  3.3 0.9 copy-done.2
  4.3 0.0 copy-start.3
  4.3 0.8 copy-done.3
  5.1 0.0 copy-start.4
  5.1 0.8 copy-done.4
  5.8 0.0 copy-start.5
  5.8 0.8 copy-done.5
  6.6 164.1 %shard_map.86 = (f32[8,64,1024]{2,1,0:T(8,128)S(1)}, f32[8,128]{1,0:T(8,128)S(1)}) custom-call(f32[64,64]{1,0:T(8,128)S(1)} %copy-done.5, f32[64,64]{1,0:T(8,128)S(1)} %copy-done.4, f32[4,3,8,128]{3,2,1,0:T(8,128)S(1)} %copy-done.3, f32[8,64,1024]{2,1,0:T(8,128)S(1)} %copy-done, f32[8,64,1024]{2,1,0:T(8,128)} %traj_ref.1, f32[64,1024]{1,0:T(8,128)S(1)} %fusion.3.base_ref, ...), custom_call_target="tpu_custom_call" | custom-call | tf_op jit(solution)/shard_map/pallas_call | solution.py:447
  170.7 0.0 copy-start.1
  170.7 1.3 copy-done.1
  172.0 0.0 copy-start.6
  172.0 0.6 copy-done.6
  172.6 6.1 %shard_map.87 = (f32[8,64,1024]{2,1,0:T(8,128)}, f32[1,1]{1,0:T(1,128)}) custom-call(f32[8,128]{1,0:T(8,128)} %copy-done.6, f32[8,64,1024]{2,1,0:T(8,128)} %copy-done.1), custom_call_target="tpu_custom_call" | custom-call | tf_op jit(solution)/shard_map/pallas_call | solution.py:466
Async XLA Ops:
  1.7 1.6 copy-start
  3.3 0.9 copy-start.2
  4.3 0.8 copy-start.3
  5.1 0.8 copy-start.4
  5.8 0.8 copy-start.5
  170.7 1.3 copy-start.1
  172.0 0.6 copy-start.6

commit v2 on v1

v2 whole, which is shorter than its diff:
```python
import functools
import math
import numpy as np
import jax
import jax.numpy as jnp
from jax import lax
from jax.experimental import pallas as pl
from jax.experimental.pallas import tpu as pltpu
from jax.sharding import PartitionSpec as P

SWEEPS = 16
DEPTH = 3
SUB = 8
LANES = 128

circ_weight = 0.2
time_step = 0.01
damping = 0.8
reaction_scale = 40.0

MESH = pl.DeviceIdType.MESH
HIGHEST = lax.Precision.HIGHEST


def time_tables(count):
    f32 = np.float32
    positions = np.arange(count, dtype=f32)
    pair_ids = np.arange(count // 2, dtype=f32)
    phases = f32(2.0 * np.pi) * pair_ids / f32(count)
    angles = phases[:, None] * positions[None, :]
    forward = np.stack([np.cos(angles), -np.sin(angles)], axis=1).reshape(count, count)
    forward[1] = np.cos(f32(np.pi) * positions)
    inverse = forward.T * np.where(np.arange(count) < 2, f32(1.0), f32(2.0)) / f32(count)
    factor = circ_weight ** (1.0 / count)
    shifts = np.repeat((1.0 - factor * np.cos(phases)) / time_step, 2)
    shifts[1] = (1.0 + factor) / time_step
    coupling = factor * np.sin(phases) / time_step
    weights = circ_weight ** (np.arange(count) / count)
    order = np.arange(count).reshape(-1, SUB, 2).transpose(0, 2, 1).reshape(count)
    forward = (forward * weights[None, :])[order]
    inverse = (inverse / weights[:, None])[:, order]
    tiles = np.stack(
        [shifts[0::2].reshape(-1, SUB), shifts[1::2].reshape(-1, SUB), -coupling.reshape(-1, SUB)], axis=1
    )
    tiles = np.broadcast_to(tiles[..., None], tiles.shape + (LANES,))
    return forward.astype(f32), inverse.astype(f32), np.ascontiguousarray(tiles, dtype=f32)


class Plan:
    def __init__(self, t_count, z_count, steps, rows, cols):
        self.t, self.z = t_count, z_count
        self.k, self.rows, self.cols = steps, rows, cols
        self.r = rows // t_count
        self.tiles = cols // LANES
        self.ring = t_count // 2

    def strip_of(self, i, z):
        chip, core = i // 2, i % 2
        half = self.ring // 2
        place = chip + (chip // half) * (self.ring + half - 1 - 2 * chip)
        return ((place + z) % self.ring) * 2 + core

    def device_of(self, strip, z):
        place, core = (strip // 2 + self.ring - z % self.ring) % self.ring, strip % 2
        half = self.ring // 2
        chip = place + (place // half) * (self.ring + half - 1 - 2 * place)
        return chip * 2 + core

    def neighbour(self, strip, z, step):
        total = self.t * self.z
        g = (z * self.t + strip + step + total) % total
        z2, s2 = g // self.t, g % self.t
        return {"tm": self.device_of(s2, z2), "space": z2}


def permuted(tiles):
    lane = lax.broadcasted_iota(jnp.int32, tiles[0].shape, 1)
    tiles, bit = list(tiles), 1
    while bit < len(tiles):
        high = (lane // bit) % 2 == 1
        for i in range(len(tiles)):
            if not i & bit:
                a, b = tiles[i], tiles[i + bit]
                tiles[i] = jnp.where(high, pltpu.roll(b, bit, 1), a)
                tiles[i + bit] = jnp.where(high, b, pltpu.roll(a, LANES - bit, 1))
        bit *= 2
    return tiles


def from_left(v, count):
    lane = lax.broadcasted_iota(jnp.int32, v.shape, 1)
    low = jnp.where(lane == 0, pltpu.roll(v, 1, 1), pltpu.roll(v, (count + 1) % LANES, 1))
    return jnp.where(lane < count, low, pltpu.roll(v, count % LANES, 1))


def from_right(v, count):
    lane = lax.broadcasted_iota(jnp.int32, v.shape, 1)
    high = jnp.where(lane == LANES - 1, pltpu.roll(v, LANES - 1, 1), pltpu.roll(v, LANES - 1 - count, 1))
    return jnp.where(lane >= LANES - count, high, pltpu.roll(v, LANES - count, 1))


def fold(v):
    total = v[:, :LANES]
    for i in range(1, v.shape[1] // LANES):
        total = total + v[:, i * LANES : (i + 1) * LANES]
    return total


def step_kernel(
    plan, phi_ref, psi_ref, tab_ref, x_hbm, traj_hbm, init_hbm, mob_hbm, dir_ref, stat_ref,
    x_ref, traj_ref, mob_ref, init_ext, mob_ext, wide_init, wide_mob, got, state, temp, gain, cross, start, out, prev,
    z_out, z_got, t_got, z_own, zs_got,
    load_sem, ext_send, ext_recv, in_send, in_recv, row_send, row_recv, back_send, back_recv,
    prev_send, prev_recv, edge_send, edge_recv, t_send, t_recv, z_send, z_recv,
):
    K, R, T, Z, CT, H = plan.k, plan.r, plan.t, plan.z, plan.tiles, DEPTH
    rows, cols = plan.rows, plan.cols
    NT = K * T
    G = NT // (2 * SUB)
    keep = 1.0 - damping
    me, z = lax.axis_index("tm"), lax.axis_index("space")
    strip = plan.strip_of(me, z)
    up, down = plan.neighbour(strip, z, -1), plan.neighbour(strip, z, 1)

    barrier = pltpu.get_barrier_semaphore()
    for i in range(1, T):
        pl.semaphore_signal(barrier, inc=1, device_id={"tm": (me + i) % T}, device_id_type=MESH)
    for i in range(1, Z):
        pl.semaphore_signal(barrier, inc=1, device_id={"space": (z + i) % Z}, device_id_type=MESH)
    for other in (up, down):
        pl.semaphore_signal(barrier, inc=1, device_id=other, device_id_type=MESH)

    loads = [
        pltpu.make_async_copy(init_hbm, init_ext.at[pl.ds(1, T)], load_sem.at[0]),
        pltpu.make_async_copy(mob_hbm, mob_ext.at[pl.ds(1, T)], load_sem.at[1]),
        pltpu.make_async_copy(x_hbm, x_ref, load_sem.at[2]),
        pltpu.make_async_copy(mob_hbm, mob_ref, load_sem.at[3]),
        pltpu.make_async_copy(traj_hbm, traj_ref, load_sem.at[4]),
    ]
    for copy in loads:
        copy.start()
    pl.semaphore_wait(barrier, T + Z)

    def lane_tile(j):
        return pl.ds(pl.multiple_of(j * LANES, LANES), LANES)

    def sent_in(j, i):
        other = (strip + i) % T
        return pltpu.make_async_remote_copy(
            src_ref=x_hbm.at[:, other, :, lane_tile(j)],
            dst_ref=got.at[j, pl.ds(me * K, K)],
            send_sem=in_send.at[j, i], recv_sem=in_recv.at[j, i],
            device_id={"tm": plan.device_of(other, z)}, device_id_type=MESH,
        )

    def send_in(j, _):
        for i in range(1, T):
            sent_in(j, i).start()
        return 0

    lax.fori_loop(0, CT, send_in, 0)

    beyond = []
    for n, (src, ext) in enumerate(((init_hbm, init_ext), (mob_hbm, mob_ext))):
        for side in range(2):
            beyond.append(
                pltpu.make_async_remote_copy(
                    src_ref=src.at[0 if side == 0 else T - 1],
                    dst_ref=ext.at[T + 1 if side == 0 else 0],
                    send_sem=ext_send.at[n, side], recv_sem=ext_recv.at[n, 1 - side],
                    device_id={"space": (z + (Z - 1 if side == 0 else 1)) % Z}, device_id_type=MESH,
                )
            )
    for copy in beyond:
        copy.start()

    for copy in loads[:3]:
        copy.wait()
    for j in range(CT):
        got[j, pl.ds(me * K, K)] = x_ref[:, strip, :, j * LANES : (j + 1) * LANES]
    for copy in beyond:
        copy.wait()

    def tile(t):
        return slice(t * LANES, (t + 1) * LANES)

    for i in range(R + 2 * (H - 1)):
        at = R + i - (H - 1)
        for ext, wide in ((init_ext, wide_init), (mob_ext, wide_mob)):
            line = ext[strip + at // R, at % R : at % R + 1, :]
            wide[i] = jnp.broadcast_to(line, (SUB, cols))

    def prepare(i, _):
        mobs, bases = [], []
        for t in range(CT):
            u, m = wide_init[i, :, tile(t)], wide_mob[i, :, tile(t)]
            mobs.append(m)
            bases.append(reaction_scale * jnp.maximum(3.0 * u * u - 1.0, 0.0) + 4.0 * m)
        mobs, bases = permuted(mobs), permuted(bases)
        for q in range(G):
            e, o = pl.ds(2 * SUB * q, SUB), pl.ds(2 * SUB * q + SUB, SUB)
            for t in range(CT):
                d_e, d_o, c = tab_ref[q, 0] + bases[t], tab_ref[q, 1] + bases[t], tab_ref[q, 2]
                scale = damping / (d_e * d_o + c * c)
                a_e, a_o, a_c = scale * d_o, scale * d_e, scale * c
                start[i, e, tile(t)] = a_e
                start[i, o, tile(t)] = a_o
                temp[i, pl.ds(SUB * q, SUB), tile(t)] = a_c
                gain[i, e, tile(t)] = a_e * mobs[t]
                gain[i, o, tile(t)] = a_o * mobs[t]
                cross[i, pl.ds(SUB * q, SUB), tile(t)] = a_c * mobs[t]
        return 0

    lax.fori_loop(0, R + 2 * (H - 1), prepare, 0)

    WIDE = 2 if CT % 2 == 0 else 1
    CH = WIDE * LANES
    strided = R % SUB == 0

    def wide_span(j):
        return pl.ds(pl.multiple_of(j * CH, LANES), CH)

    def transform(j, _):
        for w in range(WIDE):
            for i in range(1, T):
                sent_in(j * WIDE + w, i).wait()
        for r in range(R):
            if strided:
                flat = got.reshape(CT, NT * R, LANES)
                steps = [flat[j * WIDE + w, pl.ds(r, NT, stride=R), :] for w in range(WIDE)]
            else:
                steps = [got[j * WIDE + w, :, r, :] for w in range(WIDE)]
            state[0, r + H, :, wide_span(j)] = jnp.dot(
                phi_ref[...], jnp.concatenate(steps, axis=1),
                precision=HIGHEST, preferred_element_type=jnp.float32,
            )
        return 0

    lax.fori_loop(0, CT // WIDE, transform, 0)

    def group(q):
        return pl.ds(pl.multiple_of(q * 2 * SUB, 2 * SUB), 2 * SUB)

    def row_edge(slot, q, side):
        return pltpu.make_async_remote_copy(
            src_ref=state.at[slot, pl.ds(H if side == 0 else R, H), group(q)],
            dst_ref=state.at[slot, pl.ds(R + H if side == 0 else 0, H), group(q)],
            send_sem=row_send.at[slot, q, side], recv_sem=row_recv.at[slot, q, 1 - side],
            device_id=up if side == 0 else down, device_id_type=MESH,
        )

    def parts_of(q):
        at = pl.multiple_of(q * 2 * SUB, 2 * SUB)
        return pl.ds(at, SUB), pl.ds(at + SUB, SUB), pl.ds(pl.multiple_of(q * SUB, SUB), SUB)

    def first(q, _):
        e, o, c = parts_of(q)
        for r in range(R):
            s_e = permuted([state[0, r + H, e, tile(t)] for t in range(CT)])
            s_o = permuted([state[0, r + H, o, tile(t)] for t in range(CT)])
            i = r + H - 1
            for t in range(CT):
                a_e, a_o, a_c = start[i, e, tile(t)], start[i, o, tile(t)], temp[i, c, tile(t)]
                b_e = a_e * s_e[t] - a_c * s_o[t]
                b_o = a_o * s_o[t] + a_c * s_e[t]
                start[i, e, tile(t)] = b_e
                start[i, o, tile(t)] = b_o
                state[0, r + H, e, tile(t)] = b_e
                state[0, r + H, o, tile(t)] = b_o
        for side in range(2):
            row_edge(0, q, side).start()
        return 0

    lax.fori_loop(0, G, first, 0)

    rounds = (SWEEPS - 1) // H

    def visits(n, _):
        now = lax.rem(n, 2)
        later = 1 - now

        def visit(q, _):
            e, o, c_at = parts_of(q)
            for side in range(2):
                row_edge(now, q, side).wait()

            @pl.when(n == 0)
            def _():
                for r in list(range(1 - H, 0)) + list(range(R, R + H - 1)):
                    start[r + H - 1, group(q), :] = state[0, r + H, group(q), :]

            def from_state(slot):
                return lambda r, part, t: state[slot, r + H, part, tile(t)]

            def from_temp(r, part, t):
                return temp[r + H - 1, part, tile(t)]

            for i in range(1, H + 1):
                source = from_temp if i % 2 == 0 else from_state(now)
                into_temp = i % 2 == 1 and i < H
                slot = later if i == H else now
                for r in range(i - H, R + H - i):
                    y_e = [source(r, e, t) for t in range(CT)]
                    y_o = [source(r, o, t) for t in range(CT)]
                    ends = [(from_left(y[CT - 1], CT), from_right(y[0], CT)) for y in (y_e, y_o)]
                    at = r + H - 1
                    for t in range(CT):

                        def near(y, end, part):
                            low = y[t - 1] if t else end[0]
                            high = y[t + 1] if t < CT - 1 else end[1]
                            return (source(r - 1, part, t) + source(r + 1, part, t)) + (low + high)

                        n_e, n_o = near(y_e, ends[0], e), near(y_o, ends[1], o)
                        c = cross[at, c_at, tile(t)]
                        new_e = keep * y_e[t] + start[at, e, tile(t)] + (gain[at, e, tile(t)] * n_e - c * n_o)
                        new_o = keep * y_o[t] + start[at, o, tile(t)] + (gain[at, o, tile(t)] * n_o + c * n_e)
                        if into_temp:
                            temp[at, e, tile(t)] = new_e
                            temp[at, o, tile(t)] = new_o
                        else:
                            state[slot, r + H, e, tile(t)] = new_e
                            state[slot, r + H, o, tile(t)] = new_o

            @pl.when(n < rounds - 1)
            def _():
                for side in range(2):
                    row_edge(later, q, side).start()

            return 0

        return lax.fori_loop(0, G, visit, 0)

    lax.fori_loop(0, rounds, visits, 0)
    last = rounds % 2

    def unpermute(m, _):
        part = pl.ds(pl.multiple_of(m * SUB, SUB), SUB)
        for r in range(R):
            for t, v in enumerate(permuted([state[last, r + H, part, tile(t)] for t in range(CT)])):
                temp[r, part, tile(t)] = v
        return 0

    lax.fori_loop(0, NT // SUB, unpermute, 0)

    def sent_back(j, i):
        g = (me + i) % T
        return pltpu.make_async_remote_copy(
            src_ref=out.at[j, pl.ds(g * K, K)], dst_ref=dir_ref.at[:, strip, :, lane_tile(j)],
            send_sem=back_send.at[j, i], recv_sem=back_recv.at[j, i],
            device_id={"tm": g}, device_id_type=MESH,
        )

    def sent_prev(j, i):
        g = (me + i) % T
        return pltpu.make_async_remote_copy(
            src_ref=out.at[j, (g * K + NT - 1) % NT], dst_ref=prev.at[strip, :, lane_tile(j)],
            send_sem=prev_send.at[j, i], recv_sem=prev_recv.at[j, i],
            device_id={"tm": g}, device_id_type=MESH,
        )

    def restore(j, _):
        for r in range(R):
            steps = jnp.dot(
                psi_ref[...], temp[r, :, wide_span(j)],
                precision=HIGHEST, preferred_element_type=jnp.float32,
            )
            for w in range(WIDE):
                if strided:
                    flat = out.reshape(CT, NT * R, LANES)
                    flat[j * WIDE + w, pl.ds(r, NT, stride=R), :] = steps[:, tile(w)]
                else:
                    out[j * WIDE + w, :, r, :] = steps[:, tile(w)]
        for w in range(WIDE):
            for i in range(1, T):
                sent_back(j * WIDE + w, i).start()
                sent_prev(j * WIDE + w, i).start()
        return 0

    lax.fori_loop(0, CT // WIDE, restore, 0)
    for j in range(CT):
        dir_ref[:, strip, :, tile(j)] = out[j, pl.ds(me * K, K)]
        prev[strip, :, tile(j)] = out[j, (me * K + NT - 1) % NT]

    def arrive(j, _):
        for i in range(1, T):
            sent_back(j, i).wait()
            sent_prev(j, i).wait()
        return 0

    lax.fori_loop(0, CT, arrive, 0)
    for copy in loads[3:]:
        copy.wait()

    for k in range(K):
        z_out[0, k : k + 1, :] = dir_ref[k, 0, 0:1, :]
        z_out[1, k : k + 1, :] = dir_ref[k, T - 1, R - 1 : R, :]
    edges = []
    for side in range(2):
        edges.append(
            pltpu.make_async_remote_copy(
                src_ref=z_out.at[side], dst_ref=z_got.at[1 - side],
                send_sem=edge_send.at[side], recv_sem=edge_recv.at[1 - side],
                device_id={"space": (z + (Z - 1 if side == 0 else 1)) % Z}, device_id_type=MESH,
            )
        )
    for copy in edges:
        copy.start()
    sub = lax.broadcasted_iota(jnp.int32, (R, cols), 0)
    has_prev = jnp.minimum(me, 1).astype(jnp.float32)

    def shifted(v, row, side):
        if R == SUB:
            at, by = (0, 1) if side == 0 else (R - 1, R - 1)
            return jnp.where(sub == at, row, pltpu.roll(v, by, 0))
        return jnp.concatenate([row, v[: R - 1]] if side == 0 else [v[1:], row], axis=0)

    def tile_sums(k, is_first, t, acc):
        v = dir_ref[k, t]
        above = z_got[0, pl.ds(k, 1), :] if t == 0 else dir_ref[k, t - 1, R - 1 : R, :]
        below = z_got[1, pl.ds(k, 1), :] if t == T - 1 else dir_ref[k, t + 1, 0:1, :]
        near = shifted(v, above, 0) + shifted(v, below, 1) + (pltpu.roll(v, 1, 1) + pltpu.roll(v, cols - 1, 1))
        before = prev[t] * has_prev if is_first else dir_ref[k - 1, t]
        u = traj_ref[k, t]
        applied = (v - before) * (1.0 / time_step) + mob_ref[t] * (4.0 * v - near)
        applied = applied + reaction_scale * (3.0 * u * u - 1.0) * v
        res = x_ref[k, t]
        return acc[0] + fold(res * res), acc[1] + fold(res * applied), acc[2] + fold(applied * applied)

    zero = jnp.zeros((R, LANES), jnp.float32)
    acc = (zero, zero, zero)

    def some(k, is_first, which, acc):
        for t in which:
            acc = tile_sums(k, is_first, t, acc)
        return acc

    inner = list(range(1, T - 1))
    acc = some(0, True, inner, acc)
    acc = lax.fori_loop(1, K, lambda k, a: some(k, False, inner, a), acc)
    for copy in edges:
        copy.wait()
    acc = some(0, True, [0, T - 1], acc)
    acc = lax.fori_loop(1, K, lambda k, a: some(k, False, [0, T - 1], a), acc)

    row = lax.broadcasted_iota(jnp.int32, (SUB, LANES), 0)
    pack = jnp.zeros((SUB, LANES), jnp.float32)
    for n in range(3):
        pack = jnp.where(row == n, jnp.sum(acc[n], axis=0, keepdims=True), pack)
    t_got[me] = pack
    z_own[...] = pack

    def exchange(axis, count, at, dst, snd, rcv):
        copies = []
        for i in range(1, count):
            copies.append(
                pltpu.make_async_remote_copy(
                    src_ref=z_own, dst_ref=dst.at[at], send_sem=snd.at[i], recv_sem=rcv.at[i],
                    device_id={axis: (at + i) % count}, device_id_type=MESH,
                )
            )
        for copy in copies:
            copy.start()
        for copy in copies:
            copy.wait()
        total = dst[0]
        for i in range(1, count):
            total = total + dst[i]
        return total

    part = exchange("tm", T, me, t_got, t_send, t_recv)
    z_own[...] = part
    zs_got[z] = part
    total = exchange("space", Z, z, zs_got, z_send, z_recv)
    total = jnp.broadcast_to(jnp.sum(total, axis=1, keepdims=True), (SUB, LANES))
    norm, crossed, squared = total[0:1], total[1:2], total[2:3]
    projection, squared_sum = crossed / norm, squared / norm
    remainder = jnp.maximum(squared_sum - projection * projection, 0.0)
    stat_ref[0:1, :] = crossed / squared
    stat_ref[1:2, :] = jnp.sqrt(remainder / squared_sum)


def on_device(trajectory, initial_state, residual, mobility):
    t_count, z_count = lax.axis_size("tm"), lax.axis_size("space")
    steps, rows, cols = residual.shape
    plan = Plan(t_count, z_count, steps, rows, cols)
    count = steps * t_count
    groups = count // (2 * SUB)
    forward, inverse, tables = time_tables(count)
    R, H, tiles = plan.r, DEPTH, plan.tiles
    assert (SWEEPS - 1) % H == 0 and R >= H
    f32 = jnp.float32
    vmem, anywhere = pl.BlockSpec(memory_space=pltpu.VMEM), pl.BlockSpec(memory_space=pl.ANY)
    dma = pltpu.SemaphoreType.DMA
    V = lambda *shape: pltpu.VMEM(shape, f32)
    strips = (steps, t_count, R, cols)
    near = R + 2 * (H - 1)
    direction, stats = pl.pallas_call(
        functools.partial(step_kernel, plan),
        out_shape=[jax.ShapeDtypeStruct(strips, f32), jax.ShapeDtypeStruct((2, LANES), f32)],
        in_specs=[vmem] * 3 + [anywhere] * 4,
        out_specs=[vmem, vmem],
        scratch_shapes=[
            V(*strips), V(*strips), V(t_count, R, cols), V(t_count + 2, R, cols), V(t_count + 2, R, cols),
            V(near, SUB, cols), V(near, SUB, cols),
            V(tiles, count, R, LANES), V(2, R + 2 * H, count, cols), V(near, count, cols),
            V(near, count, cols), V(near, count // 2, cols), V(near, count, cols),
            V(tiles, count, R, LANES), V(t_count, R, cols), V(2, steps, cols), V(2, steps, cols),
            V(t_count, SUB, LANES), V(SUB, LANES), V(z_count, SUB, LANES),
            dma((5,)), dma((2, 2)), dma((2, 2)), dma((tiles, t_count)), dma((tiles, t_count)),
            dma((2, groups, 2)), dma((2, groups, 2)), dma((tiles, t_count)), dma((tiles, t_count)),
            dma((tiles, t_count)), dma((tiles, t_count)), dma((2,)), dma((2,)),
            dma((t_count,)), dma((t_count,)), dma((z_count,)), dma((z_count,)),
        ],
        compiler_params=pltpu.CompilerParams(
            collective_id=0, has_side_effects=True, vmem_limit_bytes=63 * 1024 * 1024
        ),
    )(
        jnp.asarray(forward), jnp.asarray(inverse), jnp.asarray(tables),
        residual.reshape(strips), trajectory.reshape(strips),
        initial_state.reshape(strips[1:]), mobility.reshape(strips[1:]),
    )
    update = stats[0:1, 0:1][None] * direction.reshape(residual.shape)
    return (update, stats[1, 0])


def solution(mesh):
    placed = (P("tm", "space", None), P("space", None), P("tm", "space", None), P("space", None))
    return jax.shard_map(
        on_device,
        mesh=mesh,
        in_specs=placed,
        out_specs=(P("tm", "space", None), P()),
        check_vma=False,
    )
```

time: 179 us -> 134 us (0.75)
  Pallas kernels: 170 us -> 128 us
  local copies, waits for them, and re-layouts: 6.78 us -> 1.28 us
  other arithmetic: 1.1 us -> 3.75 us
    pallas_call x1, Pallas kernels: 164 us -> 128 us  [on_device(): pl.pallas_call(functools.partial(step_kernel, plan), out_shape=[jax.Shape...]
    unnamed x14 -> x0, local copies, waits for them, and re-layouts: 6.78 us -> none
    pallas_call x1 -> x0, Pallas kernels: 6.06 us -> none  [on_device(): pl.pallas_call(finish_kernel, grid=(steps,), out_shape=[jax.ShapeDtypeStr...]
    mul x0 -> x1, other arithmetic: none -> 3.75 us  [on_device(): update = stats[0:1, 0:1][None] * direction.reshape(residual.shape)]
where the time goes in v2:
time: 134 us
  Pallas kernels  128 us (96%)
  other arithmetic  3.75 us (3%)
    pallas_call x1, Pallas kernels, on_device(): pl.pallas_call(functools.partial(step_kernel, plan), out_shape=[jax.Shape...  128 us
    mul x1, other arithmetic, on_device(): update = stats[0:1, 0:1][None] * direction.reshape(residual.shape)  3.75 us

profile of v2, /device:TPU:0, one launch (start us, length us, event | category | flops | bytes accessed | tf_op | source)
XLA Modules:
  0.0 133.8 jit_solution(16425498157302394628)
XLA Ops:
  0.6 128.1 %shard_map.86 = (f32[8,8,8,1024]{3,2,1,0:T(8,128)}, f32[2,128]{1,0:T(2,128)}) custom-call(f32[64,64]{1,0:T(8,128)} %constant.6.clone.phi_ref, f32[64,64]{1,0:T(8,128)} %constant.7.clone.psi_ref, f32[4,3,8,128]{3,2,1,0:T(8,128)} %constant.8.clone.tab_ref, f32[8,8,8,1024]{3,2,1,0:T(8,128)} %bitcast.8, f32[8,8,8,1024]{3,2,1,0:T(8,128)} %bitcast.9, ...), custom_call_target="tpu_custom_call" | custom-call | tf_op jit(solution)/shard_map/pallas_call | solution.py:498
  128.8 1.3 fusion
  130.1 3.7 %multiply_bitcast_fusion = f32[8,64,1024]{2,1,0:T(8,128)} fusion(f32[8,8,8,1024]{3,2,1,0:T(8,128)} %get-tuple-element.5, f32[]{:T(128)} %bitcast.4), kind=kLoop, calls=%fused_computation | loop fusion | flops 524288 | bytes 4194308 | tf_op jit(solution)/shard_map/mul | solution.py:523

commit v3 on v2

--- a/solution.py
+++ b/solution.py
@@ -107,11 +107,11 @@
 
 
 def step_kernel(
-    plan, phi_ref, psi_ref, tab_ref, x_hbm, traj_hbm, init_hbm, mob_hbm, dir_ref, stat_ref,
-    x_ref, traj_ref, mob_ref, init_ext, mob_ext, wide_init, wide_mob, got, state, temp, gain, cross, start, out, prev,
-    z_out, z_got, t_got, z_own, zs_got,
+    plan, phi_hbm, psi_hbm, tab_hbm, x_hbm, traj_hbm, init_hbm, mob_hbm, dir_ref, stat_ref,
+    phi_ref, psi_ref, tab_ref, acc, x_ref, traj_ref, mob_ref, init_ext, mob_ext, wide_init, wide_mob, got, state, temp, gain, cross, start, out, prev,
+    z_out, z_got, own_sums, all_sums,
     load_sem, ext_send, ext_recv, in_send, in_recv, row_send, row_recv, back_send, back_recv,
-    prev_send, prev_recv, edge_send, edge_recv, t_send, t_recv, z_send, z_recv,
+    prev_send, prev_recv, hand_send, hand_recv, edge_send, edge_recv, sum_send, sum_recv, column_in,
 ):
     K, R, T, Z, CT, H = plan.k, plan.r, plan.t, plan.z, plan.tiles, DEPTH
     rows, cols = plan.rows, plan.cols
@@ -134,12 +134,17 @@
         pltpu.make_async_copy(init_hbm, init_ext.at[pl.ds(1, T)], load_sem.at[0]),
         pltpu.make_async_copy(mob_hbm, mob_ext.at[pl.ds(1, T)], load_sem.at[1]),
         pltpu.make_async_copy(x_hbm, x_ref, load_sem.at[2]),
+        pltpu.make_async_copy(tab_hbm, tab_ref, load_sem.at[5]),
+        pltpu.make_async_copy(phi_hbm, phi_ref, load_sem.at[6]),
+        pltpu.make_async_copy(psi_hbm, psi_ref, load_sem.at[7]),
         pltpu.make_async_copy(mob_hbm, mob_ref, load_sem.at[3]),
         pltpu.make_async_copy(traj_hbm, traj_ref, load_sem.at[4]),
     ]
     for copy in loads:
         copy.start()
     pl.semaphore_wait(barrier, T + Z)
+    for i in range(1, T):
+        pl.semaphore_signal(column_in, inc=1, device_id={"tm": (me + i) % T}, device_id_type=MESH)
 
     def lane_tile(j):
         return pl.ds(pl.multiple_of(j * LANES, LANES), LANES)
@@ -174,7 +179,7 @@
     for copy in beyond:
         copy.start()
 
-    for copy in loads[:3]:
+    for copy in loads[:6]:
         copy.wait()
     for j in range(CT):
         got[j, pl.ds(me * K, K)] = x_ref[:, strip, :, j * LANES : (j + 1) * LANES]
@@ -359,6 +364,20 @@
             device_id={"tm": g}, device_id_type=MESH,
         )
 
+    def hand_on(j):
+        return pltpu.make_async_remote_copy(
+            src_ref=dir_ref.at[K - 1, :, :, lane_tile(j)], dst_ref=prev.at[:, :, lane_tile(j)],
+            send_sem=hand_send.at[j], recv_sem=hand_recv.at[j],
+            device_id={"tm": me + 1 - 2 * (me % 2)}, device_id_type=MESH,
+        )
+
+    def z_edge(j, side, g):
+        return pltpu.make_async_remote_copy(
+            src_ref=z_out.at[j, side, pl.ds(g * K, K)], dst_ref=z_got.at[j, 1 - side],
+            send_sem=edge_send.at[j, side, g], recv_sem=edge_recv.at[j, 1 - side],
+            device_id={"tm": g, "space": (z + (Z - 1 if side == 0 else 1)) % Z}, device_id_type=MESH,
+        )
+
     def restore(j, _):
         for r in range(R):
             steps = jnp.dot(
@@ -371,109 +390,160 @@
                     flat[j * WIDE + w, pl.ds(r, NT, stride=R), :] = steps[:, tile(w)]
                 else:
                     out[j * WIDE + w, :, r, :] = steps[:, tile(w)]
+                for side, edge in ((0, 0), (1, R - 1)):
+                    if r == edge:
+                        z_out[j * WIDE + w, side] = steps[:, tile(w)]
         for w in range(WIDE):
+            for side, edge in ((0, 0), (1, T - 1)):
+
+                @pl.when(strip == edge)
+                def _():
+                    for g in range(T):
+                        z_edge(j * WIDE + w, side, g).start()
+
             for i in range(1, T):
                 sent_back(j * WIDE + w, i).start()
-                sent_prev(j * WIDE + w, i).start()
-        return 0
-
+
+                @pl.when((me + i) % T % 2 == 0)
+                def _():
+                    sent_prev(j * WIDE + w, i).start()
+
+        return 0
+
+    pl.semaphore_wait(column_in, T - 1)
     lax.fori_loop(0, CT // WIDE, restore, 0)
+    even = me % 2 == 0
     for j in range(CT):
         dir_ref[:, strip, :, tile(j)] = out[j, pl.ds(me * K, K)]
-        prev[strip, :, tile(j)] = out[j, (me * K + NT - 1) % NT]
-
-    def arrive(j, _):
+
+    @pl.when(even)
+    def _():
+        for j in range(CT):
+            prev[strip, :, tile(j)] = out[j, (me * K + NT - 1) % NT]
+
+    for copy in loads[6:]:
+        copy.wait()
+    acc[...] = jnp.zeros_like(acc)
+
+    def arrive(j):
         for i in range(1, T):
             sent_back(j, i).wait()
-            sent_prev(j, i).wait()
-        return 0
-
-    lax.fori_loop(0, CT, arrive, 0)
-    for copy in loads[3:]:
-        copy.wait()
-
-    for k in range(K):
-        z_out[0, k : k + 1, :] = dir_ref[k, 0, 0:1, :]
-        z_out[1, k : k + 1, :] = dir_ref[k, T - 1, R - 1 : R, :]
-    edges = []
-    for side in range(2):
-        edges.append(
-            pltpu.make_async_remote_copy(
-                src_ref=z_out.at[side], dst_ref=z_got.at[1 - side],
-                send_sem=edge_send.at[side], recv_sem=edge_recv.at[1 - side],
-                device_id={"space": (z + (Z - 1 if side == 0 else 1)) % Z}, device_id_type=MESH,
-            )
-        )
-    for copy in edges:
-        copy.start()
-    sub = lax.broadcasted_iota(jnp.int32, (R, cols), 0)
+
+            @pl.when((me + i) % T % 2 == 0)
+            def _():
+                sent_prev(j, i).wait_send()
+
+        @pl.when(even)
+        def _():
+            for i in range(1, T):
+                sent_prev(j, i).wait_recv()
+            hand_on(j).start()
+
+        for side, edge in ((0, 0), (1, T - 1)):
+
+            @pl.when(strip == edge)
+            def _():
+                for g in range(T):
+                    z_edge(j, side, g).wait_send()
+
+            z_edge(j, side, me).wait_recv()
+
+    def handed(j):
+        @pl.when(even)
+        def _():
+            hand_on(j).wait_send()
+
+        @pl.when(me % 2 == 1)
+        def _():
+            hand_on(j).wait_recv()
+
+    sub = lax.broadcasted_iota(jnp.int32, (R, LANES), 0)
+    lane = lax.broadcasted_iota(jnp.int32, (R, LANES), 1)
     has_prev = jnp.minimum(me, 1).astype(jnp.float32)
 
-    def shifted(v, row, side):
+    def shifted(v, line, side):
         if R == SUB:
             at, by = (0, 1) if side == 0 else (R - 1, R - 1)
-            return jnp.where(sub == at, row, pltpu.roll(v, by, 0))
-        return jnp.concatenate([row, v[: R - 1]] if side == 0 else [v[1:], row], axis=0)
-
-    def tile_sums(k, is_first, t, acc):
-        v = dir_ref[k, t]
-        above = z_got[0, pl.ds(k, 1), :] if t == 0 else dir_ref[k, t - 1, R - 1 : R, :]
-        below = z_got[1, pl.ds(k, 1), :] if t == T - 1 else dir_ref[k, t + 1, 0:1, :]
-        near = shifted(v, above, 0) + shifted(v, below, 1) + (pltpu.roll(v, 1, 1) + pltpu.roll(v, cols - 1, 1))
-        before = prev[t] * has_prev if is_first else dir_ref[k - 1, t]
-        u = traj_ref[k, t]
-        applied = (v - before) * (1.0 / time_step) + mob_ref[t] * (4.0 * v - near)
-        applied = applied + reaction_scale * (3.0 * u * u - 1.0) * v
-        res = x_ref[k, t]
-        return acc[0] + fold(res * res), acc[1] + fold(res * applied), acc[2] + fold(applied * applied)
-
-    zero = jnp.zeros((R, LANES), jnp.float32)
-    acc = (zero, zero, zero)
-
-    def some(k, is_first, which, acc):
-        for t in which:
-            acc = tile_sums(k, is_first, t, acc)
-        return acc
-
-    inner = list(range(1, T - 1))
-    acc = some(0, True, inner, acc)
-    acc = lax.fori_loop(1, K, lambda k, a: some(k, False, inner, a), acc)
-    for copy in edges:
-        copy.wait()
-    acc = some(0, True, [0, T - 1], acc)
-    acc = lax.fori_loop(1, K, lambda k, a: some(k, False, [0, T - 1], a), acc)
-
-    row = lax.broadcasted_iota(jnp.int32, (SUB, LANES), 0)
-    pack = jnp.zeros((SUB, LANES), jnp.float32)
+            return jnp.where(sub == at, line, pltpu.roll(v, by, 0))
+        return jnp.concatenate([line, v[: R - 1]] if side == 0 else [v[1:], line], axis=0)
+
+    def tile_sums(j, k, is_first, t, sums):
+        here, west, east = lane_tile(j), lane_tile((j + CT - 1) % CT), lane_tile((j + 1) % CT)
+        v = dir_ref[k, t, :, here]
+        above = z_got[j, 0, pl.ds(k, 1), :] if t == 0 else dir_ref[k, t - 1, R - 1 : R, here]
+        below = z_got[j, 1, pl.ds(k, 1), :] if t == T - 1 else dir_ref[k, t + 1, 0:1, here]
+        low = pltpu.roll(jnp.where(lane == LANES - 1, dir_ref[k, t, :, west], v), 1, 1)
+        high = pltpu.roll(jnp.where(lane == 0, dir_ref[k, t, :, east], v), LANES - 1, 1)
+        near = (shifted(v, above, 0) + shifted(v, below, 1)) + (low + high)
+        before = prev[t, :, here] * has_prev if is_first else dir_ref[k - 1, t, :, here]
+        u = traj_ref[k, t, :, here]
+        applied = (v - before) * (1.0 / time_step) + mob_ref[t, :, here] * (4.0 * v - near)
+        applied = applied + (3.0 * reaction_scale * u * u - reaction_scale) * v
+        res = x_ref[k, t, :, here]
+        return sums[0] + res * res, sums[1] + res * applied, sums[2] + applied * applied
+
+    def add_sums(j, which):
+        def some(k, is_first, sums):
+            for t in which:
+                sums = tile_sums(j, k, is_first, t, sums)
+            return sums
+
+        sums = some(0, True, (acc[0], acc[1], acc[2]))
+        sums = lax.fori_loop(1, K, lambda k, a: some(k, False, a), sums)
+        for n in range(3):
+            acc[n] = sums[n]
+
+    arrive(0)
+    arrive(1)
+
+    def follow(j, _):
+        arrive(j)
+        handed(j - 1)
+        add_sums(j - 1, range(T))
+        return 0
+
+    lax.fori_loop(2, CT, follow, 0)
+
+    def rest(n, _):
+        j = (n + CT - 1) % CT
+        handed(j)
+        add_sums(j, range(T))
+        return 0
+
+    lax.fori_loop(0, 2, rest, 0)
+
+    at = lax.broadcasted_iota(jnp.int32, (1, LANES), 1)
+    pack = jnp.zeros((1, LANES), jnp.float32)
     for n in range(3):
-        pack = jnp.where(row == n, jnp.sum(acc[n], axis=0, keepdims=True), pack)
-    t_got[me] = pack
-    z_own[...] = pack
-
-    def exchange(axis, count, at, dst, snd, rcv):
-        copies = []
-        for i in range(1, count):
-            copies.append(
-                pltpu.make_async_remote_copy(
-                    src_ref=z_own, dst_ref=dst.at[at], send_sem=snd.at[i], recv_sem=rcv.at[i],
-                    device_id={axis: (at + i) % count}, device_id_type=MESH,
-                )
-            )
-        for copy in copies:
-            copy.start()
-        for copy in copies:
-            copy.wait()
-        total = dst[0]
-        for i in range(1, count):
-            total = total + dst[i]
-        return total
-
-    part = exchange("tm", T, me, t_got, t_send, t_recv)
-    z_own[...] = part
-    zs_got[z] = part
-    total = exchange("space", Z, z, zs_got, z_send, z_recv)
-    total = jnp.broadcast_to(jnp.sum(total, axis=1, keepdims=True), (SUB, LANES))
-    norm, crossed, squared = total[0:1], total[1:2], total[2:3]
+        pack = jnp.where(at == n, jnp.sum(acc[n]), pack)
+    own_sums[...] = pack
+    index, total_count = me * Z + z, T * Z
+    all_sums[index] = pack
+
+    def sent_sum(i):
+        other = (index + i) % total_count
+        return pltpu.make_async_remote_copy(
+            src_ref=own_sums, dst_ref=all_sums.at[index],
+            send_sem=sum_send.at[i], recv_sem=sum_recv.at[i],
+            device_id={"tm": other // Z, "space": other % Z}, device_id_type=MESH,
+        )
+
+    def send_sum(i, _):
+        sent_sum(i).start()
+        return 0
+
+    def wait_sum(i, _):
+        sent_sum(i).wait()
+        return 0
+
+    lax.fori_loop(1, total_count, send_sum, 0)
+    lax.fori_loop(1, total_count, wait_sum, 0)
+    total = all_sums[0]
+    for i in range(1, total_count):
+        total = total + all_sums[i]
+    norm, crossed, squared = [
+        jnp.broadcast_to(jnp.sum(jnp.where(at == n, total, 0.0), axis=1, keepdims=True), (1, LANES)) for n in range(3)
+    ]
     projection, squared_sum = crossed / norm, squared / norm
     remainder = jnp.maximum(squared_sum - projection * projection, 0.0)
     stat_ref[0:1, :] = crossed / squared
@@ -495,31 +565,33 @@
     V = lambda *shape: pltpu.VMEM(shape, f32)
     strips = (steps, t_count, R, cols)
     near = R + 2 * (H - 1)
-    direction, stats = pl.pallas_call(
-        functools.partial(step_kernel, plan),
-        out_shape=[jax.ShapeDtypeStruct(strips, f32), jax.ShapeDtypeStruct((2, LANES), f32)],
-        in_specs=[vmem] * 3 + [anywhere] * 4,
-        out_specs=[vmem, vmem],
-        scratch_shapes=[
-            V(*strips), V(*strips), V(t_count, R, cols), V(t_count + 2, R, cols), V(t_count + 2, R, cols),
-            V(near, SUB, cols), V(near, SUB, cols),
-            V(tiles, count, R, LANES), V(2, R + 2 * H, count, cols), V(near, count, cols),
-            V(near, count, cols), V(near, count // 2, cols), V(near, count, cols),
-            V(tiles, count, R, LANES), V(t_count, R, cols), V(2, steps, cols), V(2, steps, cols),
-            V(t_count, SUB, LANES), V(SUB, LANES), V(z_count, SUB, LANES),
-            dma((5,)), dma((2, 2)), dma((2, 2)), dma((tiles, t_count)), dma((tiles, t_count)),
-            dma((2, groups, 2)), dma((2, groups, 2)), dma((tiles, t_count)), dma((tiles, t_count)),
-            dma((tiles, t_count)), dma((tiles, t_count)), dma((2,)), dma((2,)),
-            dma((t_count,)), dma((t_count,)), dma((z_count,)), dma((z_count,)),
-        ],
-        compiler_params=pltpu.CompilerParams(
-            collective_id=0, has_side_effects=True, vmem_limit_bytes=63 * 1024 * 1024
-        ),
-    )(
+    operands = (
         jnp.asarray(forward), jnp.asarray(inverse), jnp.asarray(tables),
         residual.reshape(strips), trajectory.reshape(strips),
         initial_state.reshape(strips[1:]), mobility.reshape(strips[1:]),
     )
+    direction, stats = pl.pallas_call(
+        functools.partial(step_kernel, plan),
+        out_shape=[jax.ShapeDtypeStruct(strips, f32), jax.ShapeDtypeStruct((2, LANES), f32)],
+        in_specs=[anywhere] * 7,
+        out_specs=[vmem, vmem],
+        scratch_shapes=[
+            V(*forward.shape), V(*inverse.shape), V(*tables.shape), V(3, R, LANES), V(*strips), V(*strips), V(t_count, R, cols), V(t_count + 2, R, cols), V(t_count + 2, R, cols),
+            V(near, SUB, cols), V(near, SUB, cols),
+            V(tiles, count, R, LANES), V(2, R + 2 * H, count, cols), V(near, count, cols),
+            V(near, count, cols), V(near, count // 2, cols), V(near, count, cols),
+            V(tiles, count, R, LANES), V(t_count, R, cols), V(tiles, 2, count, LANES), V(tiles, 2, steps, LANES),
+            V(1, LANES), V(t_count * z_count, 1, LANES),
+            dma((8,)), dma((2, 2)), dma((2, 2)), dma((tiles, t_count)), dma((tiles, t_count)),
+            dma((2, groups, 2)), dma((2, groups, 2)), dma((tiles, t_count)), dma((tiles, t_count)),
+            dma((tiles, t_count)), dma((tiles, t_count)), dma((tiles,)), dma((tiles,)),
+            dma((tiles, 2, t_count)), dma((tiles, 2)),
+            dma((t_count * z_count,)), dma((t_count * z_count,)), pltpu.SemaphoreType.REGULAR,
+        ],
+        compiler_params=pltpu.CompilerParams(
+            collective_id=0, has_side_effects=True, vmem_limit_bytes=36 * 1024 * 1024
+        ),
+    )(*[pltpu.with_memory_space_constraint(v, pltpu.HBM) for v in operands])
     update = stats[0:1, 0:1][None] * direction.reshape(residual.shape)
     return (update, stats[1, 0])
 

time: 134 us -> 128 us (0.955)
  Pallas kernels: 128 us -> 124 us
  other arithmetic: 3.75 us -> 2.24 us
    pallas_call x1, Pallas kernels: 128 us -> 124 us  [on_device(): pl.pallas_call(functools.partial(step_kernel, plan), out_shape=[jax.Shape...]
    mul x1, other arithmetic: 3.75 us -> 2.24 us  [on_device(): update = stats[0:1, 0:1][None] * direction.reshape(residual.shape)]
where the time goes in v3:
time: 128 us; the launch traced here: 127 us
  Pallas kernels  124 us (97%)
  other arithmetic  2.24 us (2%)
    pallas_call x1, Pallas kernels, on_device(): pl.pallas_call(functools.partial(step_kernel, plan), out_shape=[jax.Shape...  124 us

profile of v3, /device:TPU:0, one launch (start us, length us, event | category | flops | bytes accessed | tf_op | source)
XLA Modules:
  0.0 127.4 jit_solution(1800931331339513056)
XLA Ops:
  0.6 124.0 %shard_map.86 = (f32[8,8,8,1024]{3,2,1,0:T(8,128)S(1)}, f32[2,128]{1,0:T(2,128)S(1)}) custom-call(f32[64,64]{1,0:T(8,128)} %constant.6.clone.phi_hbm, f32[64,64]{1,0:T(8,128)} %constant.7.clone.psi_hbm, f32[4,3,8,128]{3,2,1,0:T(8,128)} %constant.8.clone.tab_hbm, f32[8,8,8,1024]{3,2,1,0:T(8,128)} %bitcast.8, f32[8,8,8,1024]{3,2,1,0:T(8,128)} %bitcast.9, ...), custom_call_target="tpu_custom_call" | custom-call | tf_op jit(solution)/shard_map/pallas_call | solution.py:573
  124.6 0.5 fusion
  125.2 2.2 %multiply_bitcast_fusion = f32[8,64,1024]{2,1,0:T(8,128)} fusion(f32[8,8,8,1024]{3,2,1,0:T(8,128)S(1)} %get-tuple-element.5, f32[]{:T(128)} %bitcast.4), kind=kLoop, calls=%fused_computation | loop fusion | flops 524288 | bytes 4194308 | tf_op jit(solution)/shard_map/mul | solution.py:595

commit v4 on v3

--- a/solution.py
+++ b/solution.py
@@ -10,6 +10,8 @@
 
 SWEEPS = 16
 DEPTH = 3
+CHUNKS_IN = [4, 2, 1, 1]
+CHUNKS_OUT = [2, 2, 2, 1, 1]
 SUB = 8
 LANES = 128
 
@@ -99,11 +101,16 @@
     return jnp.where(lane >= LANES - count, high, pltpu.roll(v, LANES - count, 1))
 
 
-def fold(v):
-    total = v[:, :LANES]
-    for i in range(1, v.shape[1] // LANES):
-        total = total + v[:, i * LANES : (i + 1) * LANES]
-    return total
+def spans(sizes, count):
+    if sum(sizes) != count:
+        sizes = [1] * count
+    return [(sum(sizes[:i]), n) for i, n in enumerate(sizes)]
+
+
+def tiled(v, height):
+    rows, cols = v.shape[-2:]
+    v = v.reshape(v.shape[:-2] + (rows // height, height, cols // LANES, LANES))
+    return jnp.swapaxes(v, -3, -2)
 
 
 def step_kernel(
@@ -131,9 +138,9 @@
         pl.semaphore_signal(barrier, inc=1, device_id=other, device_id_type=MESH)
 
     loads = [
+        pltpu.make_async_copy(x_hbm, x_ref, load_sem.at[2]),
         pltpu.make_async_copy(init_hbm, init_ext.at[pl.ds(1, T)], load_sem.at[0]),
         pltpu.make_async_copy(mob_hbm, mob_ext.at[pl.ds(1, T)], load_sem.at[1]),
-        pltpu.make_async_copy(x_hbm, x_ref, load_sem.at[2]),
         pltpu.make_async_copy(tab_hbm, tab_ref, load_sem.at[5]),
         pltpu.make_async_copy(phi_hbm, phi_ref, load_sem.at[6]),
         pltpu.make_async_copy(psi_hbm, psi_ref, load_sem.at[7]),
@@ -146,24 +153,21 @@
     for i in range(1, T):
         pl.semaphore_signal(column_in, inc=1, device_id={"tm": (me + i) % T}, device_id_type=MESH)
 
-    def lane_tile(j):
-        return pl.ds(pl.multiple_of(j * LANES, LANES), LANES)
-
-    def sent_in(j, i):
+    ins, outs = spans(CHUNKS_IN, CT), spans(CHUNKS_OUT, CT)
+
+    def sent_in(n, i):
         other = (strip + i) % T
+        part = pl.ds(*ins[n])
         return pltpu.make_async_remote_copy(
-            src_ref=x_hbm.at[:, other, :, lane_tile(j)],
-            dst_ref=got.at[j, pl.ds(me * K, K)],
-            send_sem=in_send.at[j, i], recv_sem=in_recv.at[j, i],
+            src_ref=x_ref.at[:, other, part], dst_ref=got.at[pl.ds(me * K, K), part],
+            send_sem=in_send.at[n, i], recv_sem=in_recv.at[n, i],
             device_id={"tm": plan.device_of(other, z)}, device_id_type=MESH,
         )
 
-    def send_in(j, _):
+    loads[0].wait()
+    for n in range(len(ins)):
         for i in range(1, T):
-            sent_in(j, i).start()
-        return 0
-
-    lax.fori_loop(0, CT, send_in, 0)
+            sent_in(n, i).start()
 
     beyond = []
     for n, (src, ext) in enumerate(((init_hbm, init_ext), (mob_hbm, mob_ext))):
@@ -179,10 +183,9 @@
     for copy in beyond:
         copy.start()
 
-    for copy in loads[:6]:
+    for copy in loads[1:6]:
         copy.wait()
-    for j in range(CT):
-        got[j, pl.ds(me * K, K)] = x_ref[:, strip, :, j * LANES : (j + 1) * LANES]
+    got[pl.ds(me * K, K)] = x_ref[:, strip]
     for copy in beyond:
         copy.wait()
 
@@ -192,8 +195,9 @@
     for i in range(R + 2 * (H - 1)):
         at = R + i - (H - 1)
         for ext, wide in ((init_ext, wide_init), (mob_ext, wide_mob)):
-            line = ext[strip + at // R, at % R : at % R + 1, :]
-            wide[i] = jnp.broadcast_to(line, (SUB, cols))
+            for t in range(CT):
+                line = ext[strip + at // R, t, at % R : at % R + 1, :]
+                wide[i, :, t * LANES : (t + 1) * LANES] = jnp.broadcast_to(line, (SUB, LANES))
 
     def prepare(i, _):
         mobs, bases = [], []
@@ -218,30 +222,38 @@
 
     lax.fori_loop(0, R + 2 * (H - 1), prepare, 0)
 
-    WIDE = 2 if CT % 2 == 0 else 1
-    CH = WIDE * LANES
     strided = R % SUB == 0
 
-    def wide_span(j):
-        return pl.ds(pl.multiple_of(j * CH, LANES), CH)
-
-    def transform(j, _):
-        for w in range(WIDE):
-            for i in range(1, T):
-                sent_in(j * WIDE + w, i).wait()
-        for r in range(R):
-            if strided:
-                flat = got.reshape(CT, NT * R, LANES)
-                steps = [flat[j * WIDE + w, pl.ds(r, NT, stride=R), :] for w in range(WIDE)]
-            else:
-                steps = [got[j * WIDE + w, :, r, :] for w in range(WIDE)]
-            state[0, r + H, :, wide_span(j)] = jnp.dot(
-                phi_ref[...], jnp.concatenate(steps, axis=1),
-                precision=HIGHEST, preferred_element_type=jnp.float32,
-            )
-        return 0
-
-    lax.fori_loop(0, CT // WIDE, transform, 0)
+    def lane_tile(j):
+        return pl.ds(pl.multiple_of(j * LANES, LANES), LANES)
+
+    def width(tiles):
+        return 2 if tiles % 2 == 0 else 1
+
+    for n, (base, tiles) in enumerate(ins):
+        for i in range(1, T):
+            sent_in(n, i).wait()
+        wide = width(tiles)
+
+        def transform(m, _, base=base, wide=wide):
+            for r in range(R):
+                steps = []
+                for w in range(wide):
+                    j = base + m * wide + w
+                    if strided:
+                        flat = got.reshape(NT * CT * R, LANES)
+                        steps.append(flat[pl.ds(j * R + r, NT, stride=CT * R), :])
+                    else:
+                        steps.append(got[:, j, r, :])
+                spec = jnp.dot(
+                    phi_ref[...], jnp.concatenate(steps, axis=1),
+                    precision=HIGHEST, preferred_element_type=jnp.float32,
+                )
+                for w in range(wide):
+                    state[0, r + H, :, lane_tile(base + m * wide + w)] = spec[:, tile(w)]
+            return 0
+
+        lax.fori_loop(0, tiles // wide, transform, 0)
 
     def group(q):
         return pl.ds(pl.multiple_of(q * 2 * SUB, 2 * SUB), 2 * SUB)
@@ -279,9 +291,10 @@
     lax.fori_loop(0, G, first, 0)
 
     rounds = (SWEEPS - 1) // H
-
-    def visits(n, _):
-        now = lax.rem(n, 2)
+    final_out = start
+
+    def visits(n, final):
+        now = n % 2
         later = 1 - now
 
         def visit(q, _):
@@ -289,10 +302,12 @@
             for side in range(2):
                 row_edge(now, q, side).wait()
 
-            @pl.when(n == 0)
-            def _():
-                for r in list(range(1 - H, 0)) + list(range(R, R + H - 1)):
-                    start[r + H - 1, group(q), :] = state[0, r + H, group(q), :]
+            if not final:
+
+                @pl.when(n == 0)
+                def _():
+                    for r in list(range(1 - H, 0)) + list(range(R, R + H - 1)):
+                        start[r + H - 1, group(q), :] = state[0, r + H, group(q), :]
 
             def from_state(slot):
                 return lambda r, part, t: state[slot, r + H, part, tile(t)]
@@ -309,6 +324,7 @@
                     y_o = [source(r, o, t) for t in range(CT)]
                     ends = [(from_left(y[CT - 1], CT), from_right(y[0], CT)) for y in (y_e, y_o)]
                     at = r + H - 1
+                    ready = []
                     for t in range(CT):
 
                         def near(y, end, part):
@@ -320,15 +336,20 @@
                         c = cross[at, c_at, tile(t)]
                         new_e = keep * y_e[t] + start[at, e, tile(t)] + (gain[at, e, tile(t)] * n_e - c * n_o)
                         new_o = keep * y_o[t] + start[at, o, tile(t)] + (gain[at, o, tile(t)] * n_o + c * n_e)
-                        if into_temp:
+                        if final and i == H:
+                            ready.append((new_e, new_o))
+                        elif into_temp:
                             temp[at, e, tile(t)] = new_e
                             temp[at, o, tile(t)] = new_o
                         else:
                             state[slot, r + H, e, tile(t)] = new_e
                             state[slot, r + H, o, tile(t)] = new_o
-
-            @pl.when(n < rounds - 1)
-            def _():
+                    if ready:
+                        for n_part, part in enumerate((e, o)):
+                            for t, v in enumerate(permuted([pair[n_part] for pair in ready])):
+                                final_out[r, part, tile(t)] = v
+
+            if not final:
                 for side in range(2):
                     row_edge(later, q, side).start()
 
@@ -336,90 +357,87 @@
 
         return lax.fori_loop(0, G, visit, 0)
 
-    lax.fori_loop(0, rounds, visits, 0)
-    last = rounds % 2
-
-    def unpermute(m, _):
-        part = pl.ds(pl.multiple_of(m * SUB, SUB), SUB)
-        for r in range(R):
-            for t, v in enumerate(permuted([state[last, r + H, part, tile(t)] for t in range(CT)])):
-                temp[r, part, tile(t)] = v
-        return 0
-
-    lax.fori_loop(0, NT // SUB, unpermute, 0)
-
-    def sent_back(j, i):
+    lax.fori_loop(0, rounds - 1, lambda n, _: visits(n, False), 0)
+    visits(rounds - 1, True)
+
+    def sent_back(n, i):
         g = (me + i) % T
+        part = pl.ds(*outs[n])
         return pltpu.make_async_remote_copy(
-            src_ref=out.at[j, pl.ds(g * K, K)], dst_ref=dir_ref.at[:, strip, :, lane_tile(j)],
-            send_sem=back_send.at[j, i], recv_sem=back_recv.at[j, i],
+            src_ref=out.at[pl.ds(g * K, K), part], dst_ref=dir_ref.at[:, strip, part],
+            send_sem=back_send.at[n, i], recv_sem=back_recv.at[n, i],
             device_id={"tm": g}, device_id_type=MESH,
         )
 
-    def sent_prev(j, i):
+    def sent_prev(n, i):
         g = (me + i) % T
+        part = pl.ds(*outs[n])
         return pltpu.make_async_remote_copy(
-            src_ref=out.at[j, (g * K + NT - 1) % NT], dst_ref=prev.at[strip, :, lane_tile(j)],
-            send_sem=prev_send.at[j, i], recv_sem=prev_recv.at[j, i],
+            src_ref=out.at[(g * K + NT - 1) % NT, part], dst_ref=prev.at[strip, part],
+            send_sem=prev_send.at[n, i], recv_sem=prev_recv.at[n, i],
             device_id={"tm": g}, device_id_type=MESH,
         )
 
-    def hand_on(j):
+    def hand_on(n):
+        part = pl.ds(*outs[n])
         return pltpu.make_async_remote_copy(
-            src_ref=dir_ref.at[K - 1, :, :, lane_tile(j)], dst_ref=prev.at[:, :, lane_tile(j)],
-            send_sem=hand_send.at[j], recv_sem=hand_recv.at[j],
+            src_ref=dir_ref.at[K - 1, :, part], dst_ref=prev.at[:, part],
+            send_sem=hand_send.at[n], recv_sem=hand_recv.at[n],
             device_id={"tm": me + 1 - 2 * (me % 2)}, device_id_type=MESH,
         )
 
-    def z_edge(j, side, g):
+    def z_edge(n, side, g):
+        part = pl.ds(*outs[n])
         return pltpu.make_async_remote_copy(
-            src_ref=z_out.at[j, side, pl.ds(g * K, K)], dst_ref=z_got.at[j, 1 - side],
-            send_sem=edge_send.at[j, side, g], recv_sem=edge_recv.at[j, 1 - side],
+            src_ref=z_out.at[side, part, pl.ds(g * K, K)], dst_ref=z_got.at[1 - side, part],
+            send_sem=edge_send.at[n, side, g], recv_sem=edge_recv.at[n, 1 - side],
             device_id={"tm": g, "space": (z + (Z - 1 if side == 0 else 1)) % Z}, device_id_type=MESH,
         )
 
-    def restore(j, _):
-        for r in range(R):
-            steps = jnp.dot(
-                psi_ref[...], temp[r, :, wide_span(j)],
-                precision=HIGHEST, preferred_element_type=jnp.float32,
-            )
-            for w in range(WIDE):
-                if strided:
-                    flat = out.reshape(CT, NT * R, LANES)
-                    flat[j * WIDE + w, pl.ds(r, NT, stride=R), :] = steps[:, tile(w)]
-                else:
-                    out[j * WIDE + w, :, r, :] = steps[:, tile(w)]
-                for side, edge in ((0, 0), (1, R - 1)):
-                    if r == edge:
-                        z_out[j * WIDE + w, side] = steps[:, tile(w)]
-        for w in range(WIDE):
-            for side, edge in ((0, 0), (1, T - 1)):
-
-                @pl.when(strip == edge)
-                def _():
-                    for g in range(T):
-                        z_edge(j * WIDE + w, side, g).start()
-
-            for i in range(1, T):
-                sent_back(j * WIDE + w, i).start()
-
-                @pl.when((me + i) % T % 2 == 0)
-                def _():
-                    sent_prev(j * WIDE + w, i).start()
-
-        return 0
-
     pl.semaphore_wait(column_in, T - 1)
-    lax.fori_loop(0, CT // WIDE, restore, 0)
+    for n, (base, tiles) in enumerate(outs):
+        wide = width(tiles)
+
+        def restore(m, _, base=base, wide=wide):
+            first = base + m * wide
+            for r in range(R):
+                steps = jnp.dot(
+                    psi_ref[...], final_out[r, :, pl.ds(pl.multiple_of(first * LANES, LANES), wide * LANES)],
+                    precision=HIGHEST, preferred_element_type=jnp.float32,
+                )
+                for w in range(wide):
+                    j = first + w
+                    if strided:
+                        flat = out.reshape(NT * CT * R, LANES)
+                        flat[pl.ds(j * R + r, NT, stride=CT * R), :] = steps[:, tile(w)]
+                    else:
+                        out[:, j, r, :] = steps[:, tile(w)]
+                    for side, edge in ((0, 0), (1, R - 1)):
+                        if r == edge:
+                            z_out[side, j] = steps[:, tile(w)]
+            return 0
+
+        lax.fori_loop(0, tiles // wide, restore, 0)
+        for side, edge in ((0, 0), (1, T - 1)):
+
+            @pl.when(strip == edge)
+            def _():
+                for g in range(T):
+                    z_edge(n, side, g).start()
+
+        for i in range(1, T):
+            sent_back(n, i).start()
+
+            @pl.when((me + i) % T % 2 == 0)
+            def _():
+                sent_prev(n, i).start()
+
     even = me % 2 == 0
-    for j in range(CT):
-        dir_ref[:, strip, :, tile(j)] = out[j, pl.ds(me * K, K)]
+    dir_ref[:, strip] = out[pl.ds(me * K, K)]
 
     @pl.when(even)
     def _():
-        for j in range(CT):
-            prev[strip, :, tile(j)] = out[j, (me * K + NT - 1) % NT]
+        prev[strip] = out[(me * K + NT - 1) % NT]
 
     for copy in loads[6:]:
         copy.wait()
@@ -468,18 +486,18 @@
         return jnp.concatenate([line, v[: R - 1]] if side == 0 else [v[1:], line], axis=0)
 
     def tile_sums(j, k, is_first, t, sums):
-        here, west, east = lane_tile(j), lane_tile((j + CT - 1) % CT), lane_tile((j + 1) % CT)
-        v = dir_ref[k, t, :, here]
-        above = z_got[j, 0, pl.ds(k, 1), :] if t == 0 else dir_ref[k, t - 1, R - 1 : R, here]
-        below = z_got[j, 1, pl.ds(k, 1), :] if t == T - 1 else dir_ref[k, t + 1, 0:1, here]
-        low = pltpu.roll(jnp.where(lane == LANES - 1, dir_ref[k, t, :, west], v), 1, 1)
-        high = pltpu.roll(jnp.where(lane == 0, dir_ref[k, t, :, east], v), LANES - 1, 1)
+        west, east = (j + CT - 1) % CT, (j + 1) % CT
+        v = dir_ref[k, t, j]
+        above = z_got[0, j, pl.ds(k, 1), :] if t == 0 else dir_ref[k, t - 1, j, R - 1 : R, :]
+        below = z_got[1, j, pl.ds(k, 1), :] if t == T - 1 else dir_ref[k, t + 1, j, 0:1, :]
+        low = pltpu.roll(jnp.where(lane == LANES - 1, dir_ref[k, t, west], v), 1, 1)
+        high = pltpu.roll(jnp.where(lane == 0, dir_ref[k, t, east], v), LANES - 1, 1)
         near = (shifted(v, above, 0) + shifted(v, below, 1)) + (low + high)
-        before = prev[t, :, here] * has_prev if is_first else dir_ref[k - 1, t, :, here]
-        u = traj_ref[k, t, :, here]
-        applied = (v - before) * (1.0 / time_step) + mob_ref[t, :, here] * (4.0 * v - near)
+        before = prev[t, j] * has_prev if is_first else dir_ref[k - 1, t, j]
+        u = traj_ref[k, t, j]
+        applied = (v - before) * (1.0 / time_step) + mob_ref[t, j] * (4.0 * v - near)
         applied = applied + (3.0 * reaction_scale * u * u - reaction_scale) * v
-        res = x_ref[k, t, :, here]
+        res = x_ref[k, t, j]
         return sums[0] + res * res, sums[1] + res * applied, sums[2] + applied * applied
 
     def add_sums(j, which):
@@ -492,30 +510,24 @@
         sums = lax.fori_loop(1, K, lambda k, a: some(k, False, a), sums)
         for n in range(3):
             acc[n] = sums[n]
-
-    arrive(0)
-    arrive(1)
-
-    def follow(j, _):
-        arrive(j)
-        handed(j - 1)
-        add_sums(j - 1, range(T))
         return 0
 
-    lax.fori_loop(2, CT, follow, 0)
-
-    def rest(n, _):
-        j = (n + CT - 1) % CT
-        handed(j)
-        add_sums(j, range(T))
-        return 0
-
-    lax.fori_loop(0, 2, rest, 0)
-
-    at = lax.broadcasted_iota(jnp.int32, (1, LANES), 1)
-    pack = jnp.zeros((1, LANES), jnp.float32)
+    def tiles_sums(low, high):
+        if high > low:
+            lax.fori_loop(low, high, lambda j, _: add_sums(j % CT, range(T)), 0)
+
+    for n, (base, tiles) in enumerate(outs):
+        arrive(n)
+        if n:
+            handed(n - 1)
+            tiles_sums(max(outs[n - 1][0], 1), base)
+    handed(len(outs) - 1)
+    tiles_sums(outs[-1][0], CT + 1)
+
+    at = lax.broadcasted_iota(jnp.int32, (SUB, LANES), 0)
+    pack = jnp.zeros((SUB, LANES), jnp.float32)
     for n in range(3):
-        pack = jnp.where(at == n, jnp.sum(acc[n]), pack)
+        pack = jnp.where(at == n, jnp.sum(acc[n], axis=0, keepdims=True), pack)
     own_sums[...] = pack
     index, total_count = me * Z + z, T * Z
     all_sums[index] = pack
@@ -541,12 +553,20 @@
     total = all_sums[0]
     for i in range(1, total_count):
         total = total + all_sums[i]
-    norm, crossed, squared = [
-        jnp.broadcast_to(jnp.sum(jnp.where(at == n, total, 0.0), axis=1, keepdims=True), (1, LANES)) for n in range(3)
-    ]
+    total = jnp.broadcast_to(jnp.sum(total, axis=1, keepdims=True), (SUB, LANES))
+    norm, crossed, squared = total[0:1], total[1:2], total[2:3]
     projection, squared_sum = crossed / norm, squared / norm
     remainder = jnp.maximum(squared_sum - projection * projection, 0.0)
     stat_ref[0:1, :] = crossed / squared
+    alpha = jnp.broadcast_to(crossed / squared, (R, LANES))
+
+    def scaled(k, _):
+        for t in range(T):
+            for j in range(CT):
+                dir_ref[k, t, j] = alpha * dir_ref[k, t, j]
+        return 0
+
+    lax.fori_loop(0, K, scaled, 0)
     stat_ref[1:2, :] = jnp.sqrt(remainder / squared_sum)
 
 
@@ -563,12 +583,11 @@
     vmem, anywhere = pl.BlockSpec(memory_space=pltpu.VMEM), pl.BlockSpec(memory_space=pl.ANY)
     dma = pltpu.SemaphoreType.DMA
     V = lambda *shape: pltpu.VMEM(shape, f32)
-    strips = (steps, t_count, R, cols)
+    strips = (steps, t_count, tiles, R, LANES)
     near = R + 2 * (H - 1)
     operands = (
         jnp.asarray(forward), jnp.asarray(inverse), jnp.asarray(tables),
-        residual.reshape(strips), trajectory.reshape(strips),
-        initial_state.reshape(strips[1:]), mobility.reshape(strips[1:]),
+        tiled(residual, R), tiled(trajectory, R), tiled(initial_state, R), tiled(mobility, R),
     )
     direction, stats = pl.pallas_call(
         functools.partial(step_kernel, plan),
@@ -576,12 +595,12 @@
         in_specs=[anywhere] * 7,
         out_specs=[vmem, vmem],
         scratch_shapes=[
-            V(*forward.shape), V(*inverse.shape), V(*tables.shape), V(3, R, LANES), V(*strips), V(*strips), V(t_count, R, cols), V(t_count + 2, R, cols), V(t_count + 2, R, cols),
+            V(*forward.shape), V(*inverse.shape), V(*tables.shape), V(3, R, LANES), V(*strips), V(*strips), V(*strips[1:]), V(t_count + 2, *strips[2:]), V(t_count + 2, *strips[2:]),
             V(near, SUB, cols), V(near, SUB, cols),
-            V(tiles, count, R, LANES), V(2, R + 2 * H, count, cols), V(near, count, cols),
+            V(count, tiles, R, LANES), V(2, R + 2 * H, count, cols), V(near, count, cols),
             V(near, count, cols), V(near, count // 2, cols), V(near, count, cols),
-            V(tiles, count, R, LANES), V(t_count, R, cols), V(tiles, 2, count, LANES), V(tiles, 2, steps, LANES),
-            V(1, LANES), V(t_count * z_count, 1, LANES),
+            V(count, tiles, R, LANES), V(*strips[1:]), V(2, tiles, count, LANES), V(2, tiles, steps, LANES),
+            V(SUB, LANES), V(t_count * z_count, SUB, LANES),
             dma((8,)), dma((2, 2)), dma((2, 2)), dma((tiles, t_count)), dma((tiles, t_count)),
             dma((2, groups, 2)), dma((2, groups, 2)), dma((tiles, t_count)), dma((tiles, t_count)),
             dma((tiles, t_count)), dma((tiles, t_count)), dma((tiles,)), dma((tiles,)),
@@ -592,7 +611,7 @@
             collective_id=0, has_side_effects=True, vmem_limit_bytes=36 * 1024 * 1024
         ),
     )(*[pltpu.with_memory_space_constraint(v, pltpu.HBM) for v in operands])
-    update = stats[0:1, 0:1][None] * direction.reshape(residual.shape)
+    update = jnp.swapaxes(direction, -3, -2).reshape(residual.shape)
     return (update, stats[1, 0])
 
 

time: 128 us -> 126 us (0.984)
  other arithmetic: 2.24 us -> 0 us
  local copies, waits for them, and re-layouts: 0.54 us -> 1.83 us
    mul x1 -> x0, other arithmetic: 2.24 us -> none  [on_device(): update = stats[0:1, 0:1][None] * direction.reshape(residual.shape)]
    unnamed x0 -> x1, local copies, waits for them, and re-layouts: none -> 1.32 us
where the time goes in v4:
time: 126 us
  Pallas kernels  124 us (98%)
  local copies, waits for them, and re-layouts  1.83 us (1%)
    pallas_call x1, Pallas kernels, on_device(): pl.pallas_call(functools.partial(step_kernel, plan), out_shape=[jax.Shape...  124 us

profile of v4, /device:TPU:0, one launch (start us, length us, event | category | flops | bytes accessed | tf_op | source)
XLA Modules:
  0.0 126.1 jit_solution(17334979542637581280)
XLA Ops:
  0.6 123.7 %shard_map.86 = (f32[8,8,8,8,128]{4,3,2,1,0:T(8,128)S(1)}, f32[2,128]{1,0:T(2,128)S(1)}) custom-call(f32[64,64]{1,0:T(8,128)} %constant.6.clone.phi_hbm, f32[64,64]{1,0:T(8,128)} %constant.7.clone.psi_hbm, f32[4,3,8,128]{3,2,1,0:T(8,128)} %constant.8.clone.tab_hbm, f32[8,8,8,8,128]{4,3,2,1,0:T(8,128)} %bitcast.17, f32[8,8,8,8,128]{4,3,2,1,0:T(8,128)} %bitcast.18, ...), custom_call_target="tpu_custom_call" | custom-call | tf_op jit(solution)/shard_map/pallas_call | solution.py:592
  124.3 0.5 slice.3
  124.8 1.3 %copy.10 = f32[8,64,1024]{2,1,0:T(8,128)} copy(f32[8,64,1024]{2,1,0:T(8,128)S(1)} %bitcast.16) | data formatting | bytes 4194304

commit v5 on v4

--- a/solution.py
+++ b/solution.py
@@ -488,8 +488,8 @@
     def tile_sums(j, k, is_first, t, sums):
         west, east = (j + CT - 1) % CT, (j + 1) % CT
         v = dir_ref[k, t, j]
-        above = z_got[0, j, pl.ds(k, 1), :] if t == 0 else dir_ref[k, t - 1, j, R - 1 : R, :]
-        below = z_got[1, j, pl.ds(k, 1), :] if t == T - 1 else dir_ref[k, t + 1, j, 0:1, :]
+        above = z_got[0, j, k : k + 1, :] if t == 0 else dir_ref[k, t - 1, j, R - 1 : R, :]
+        below = z_got[1, j, k : k + 1, :] if t == T - 1 else dir_ref[k, t + 1, j, 0:1, :]
         low = pltpu.roll(jnp.where(lane == LANES - 1, dir_ref[k, t, west], v), 1, 1)
         high = pltpu.roll(jnp.where(lane == 0, dir_ref[k, t, east], v), LANES - 1, 1)
         near = (shifted(v, above, 0) + shifted(v, below, 1)) + (low + high)
@@ -507,7 +507,8 @@
             return sums
 
         sums = some(0, True, (acc[0], acc[1], acc[2]))
-        sums = lax.fori_loop(1, K, lambda k, a: some(k, False, a), sums)
+        for k in range(1, K):
+            sums = some(k, False, sums)
         for n in range(3):
             acc[n] = sums[n]
         return 0
@@ -548,8 +549,10 @@
         sent_sum(i).wait()
         return 0
 
-    lax.fori_loop(1, total_count, send_sum, 0)
-    lax.fori_loop(1, total_count, wait_sum, 0)
+    for i in range(1, total_count):
+        sent_sum(i).start()
+    for i in range(1, total_count):
+        sent_sum(i).wait()
     total = all_sums[0]
     for i in range(1, total_count):
         total = total + all_sums[i]

time: 126 us -> 125 us (level)
  no operation moved by 1% of the time
where the time goes in v5:
time: 125 us
  Pallas kernels  123 us (98%)
  local copies, waits for them, and re-layouts  1.83 us (1%)
    pallas_call x1, Pallas kernels, on_device(): pl.pallas_call(functools.partial(step_kernel, plan), out_shape=[jax.Shape...  123 us

profile of v5, /device:TPU:0, one launch (start us, length us, event | category | flops | bytes accessed | tf_op | source)
XLA Modules:
  0.0 125.1 jit_solution(10366447679529023089)
XLA Ops:
  0.6 122.7 %shard_map.86 = (f32[8,8,8,8,128]{4,3,2,1,0:T(8,128)S(1)}, f32[2,128]{1,0:T(2,128)S(1)}) custom-call(f32[64,64]{1,0:T(8,128)} %constant.6.clone.phi_hbm, f32[64,64]{1,0:T(8,128)} %constant.7.clone.psi_hbm, f32[4,3,8,128]{3,2,1,0:T(8,128)} %constant.8.clone.tab_hbm, f32[8,8,8,8,128]{4,3,2,1,0:T(8,128)} %bitcast.17, f32[8,8,8,8,128]{4,3,2,1,0:T(8,128)} %bitcast.18, ...), custom_call_target="tpu_custom_call" | custom-call | tf_op jit(solution)/shard_map/pallas_call | solution.py:595
  123.3 0.5 slice.3
  123.8 1.3 %copy.10 = f32[8,64,1024]{2,1,0:T(8,128)} copy(f32[8,64,1024]{2,1,0:T(8,128)S(1)} %bitcast.16) | data formatting | bytes 4194304
